TPU v7x, 256 devices: a whole 4x4x8 slice. The times are simulated.
256 devices in a mesh: dp: 16 (over x, y), mp: 16 (over z, core).
Axes of the slice: x: 4, y: 4, z: 8, core: 2. Of those that a mesh axis runs over, the one named last changes fastest.
Arguments:
- query_grads: bfloat16 [16, 1, 3584, 4096], P('dp', None, None, 'mp'), may hold values from -102 to 102
- merge_grads: bfloat16 [16, 1, 4096, 3584], P('dp', None, 'mp'), may hold values from -102 to 102
- query_accum: float32 [1, 3584, 4096], P(None, 'dp', 'mp'), may hold values from -406 to 406
- merge_accum: float32 [1, 4096, 3584], P(None, 'mp', 'dp'), may hold values from -406 to 406
- query_master: float32 [1, 3584, 4096], P(None, 'dp', 'mp'), may hold values from -0.75 to 0.75
- merge_master: float32 [1, 4096, 3584], P(None, 'mp', 'dp'), may hold values from -0.75 to 0.75
- query_moment: float32 [1, 3584, 4096], P(None, 'dp', 'mp'), may hold values from -6 to 6
- merge_moment: float32 [1, 4096, 3584], P(None, 'mp', 'dp'), may hold values from -6 to 6
- query_second: float32 [1, 3584, 4096], P(None, 'dp', 'mp'), may hold values from 0.3 to 3
- merge_second: float32 [1, 4096, 3584], P(None, 'mp', 'dp'), may hold values from 0.3 to 3
Outputs:
- query_weight: bfloat16 [1, 3584, 4096], P(None, None, 'mp')
- merge_weight: bfloat16 [1, 4096, 3584], P(None, 'mp')
- query_shard: float32 [1, 3584, 4096], P(None, 'dp', 'mp')
- merge_shard: float32 [1, 4096, 3584], P(None, 'mp', 'dp')
- query_first: float32 [1, 3584, 4096], P(None, 'dp', 'mp')
- merge_first: float32 [1, 4096, 3584], P(None, 'mp', 'dp')
- query_variance: float32 [1, 3584, 4096], P(None, 'dp', 'mp')
- merge_variance: float32 [1, 4096, 3584], P(None, 'mp', 'dp')
All inputs are finite; a program needn't handle non-finite values.
Results may differ from a plain program's by a relative error of at most 0.0015.
Values may be sent and summed in bfloat16 or wider, within the bound.
A program may use at most 64 MiB of HBM per device.

v0:
```python
import jax
import jax.numpy as jnp
from jax import lax
from jax.sharding import Mesh
from jax.sharding import PartitionSpec as P

STEP = 10
ENTRIES = 29360128
DP = ("dp_0", "dp_1")
DP_MP = ("dp_0", "dp_1", "mp_0", "mp_1")
MP = ("mp_0", "mp_1")


beta_one = 0.9
beta_two = 0.95
learn_rate = 0.002
weight_decay = 0.1
adam_eps = 1e-08


def by_axis(value, axes):
    for axis in axes:
        value = lax.psum(value, axis)
    return value


def turned_gather(arrays, axis, dims):
    turned = [jnp.moveaxis(a, dim, 0) for a, dim in zip(arrays, dims)]
    widths = [t[0].size for t in turned]
    both = jnp.concatenate([t.reshape(-1, w) for t, w in zip(turned, widths)], axis=1)
    out = lax.all_gather(both, axis, axis=0, tiled=True)
    pieces = jnp.split(out, [sum(widths[:k]) for k in range(1, len(widths))], axis=1)
    return tuple(
        (
            jnp.moveaxis(b.reshape(-1, *t.shape[1:]), 0, dim)
            for b, t, dim in zip(pieces, turned, dims)
        )
    )


def adamw(total, clip, master, moment, second):
    scaled = clip * total
    first = beta_one * moment + (1.0 - beta_one) * scaled
    variance = beta_two * second + (1.0 - beta_two) * scaled * scaled
    corr_one = 1.0 - beta_one**STEP
    corr_two = 1.0 - beta_two**STEP
    update = first / corr_one / (jnp.sqrt(variance / corr_two) + adam_eps) + weight_decay * master
    return (master - learn_rate * update, first, variance)


def on_device(
    query_grads,
    merge_grads,
    query_accum,
    merge_accum,
    query_master,
    merge_master,
    query_moment,
    merge_moment,
    query_second,
    merge_second,
):
    layers = query_grads.shape[1]
    width = query_grads.shape[2]
    heads_local = query_grads.shape[3]
    owners = lax.axis_size(DP)
    query_flat = query_grads[0].reshape(layers, owners, width // owners * heads_local)
    merge_flat = merge_grads[0].reshape(layers * heads_local, owners, width // owners)
    query_parts, merge_parts = (
        lax.all_to_all(query_flat, DP, split_axis=1, concat_axis=1, tiled=True),
        lax.all_to_all(merge_flat, DP, split_axis=1, concat_axis=1, tiled=True),
    )
    query_sum = jnp.sum(query_parts, axis=1, dtype=jnp.float32).reshape(
        layers, width // owners, heads_local
    )
    merge_sum = jnp.sum(merge_parts, axis=1, dtype=jnp.float32).reshape(
        layers, heads_local, width // owners
    )
    query_total = query_accum + query_sum
    merge_total = merge_accum + merge_sum
    local_squares = jnp.sum(query_total * query_total) + jnp.sum(merge_total * merge_total)
    sumsq = by_axis(local_squares, DP_MP)
    clip = jnp.minimum(1.0, lax.rsqrt(sumsq / float(ENTRIES) + 1e-06))
    query_shard, query_first, query_variance = adamw(
        query_total, clip, query_master, query_moment, query_second
    )
    merge_shard, merge_first, merge_variance = adamw(
        merge_total, clip, merge_master, merge_moment, merge_second
    )
    query_weight, merge_weight = turned_gather(
        (query_shard.astype(jnp.bfloat16), merge_shard.astype(jnp.bfloat16)), DP, (1, 2)
    )
    return (
        query_weight,
        merge_weight,
        query_shard,
        merge_shard,
        query_first,
        merge_first,
        query_variance,
        merge_variance,
    )


def solution(mesh):
    finer = Mesh(mesh.devices.reshape(4, 4, 8, 2), ("dp_0", "dp_1", "mp_0", "mp_1"))
    placed = (
        P(DP, None, None, MP),
        P(DP, None, MP, None),
        P(None, DP, MP),
        P(None, MP, DP),
        P(None, DP, MP),
        P(None, MP, DP),
        P(None, DP, MP),
        P(None, MP, DP),
        P(None, DP, MP),
        P(None, MP, DP),
    )
    return jax.shard_map(
        on_device,
        mesh=finer,
        in_specs=placed,
        out_specs=(
            P(None, None, MP),
            P(None, MP, None),
            P(None, DP, MP),
            P(None, MP, DP),
            P(None, DP, MP),
            P(None, MP, DP),
            P(None, DP, MP),
            P(None, MP, DP),
        ),
        check_vma=False,
    )
```

profile of v0, /device:TPU:8, one launch (start us, length us, event | category | flops | bytes accessed | tf_op | source)
XLA Modules:
  0.0 202.1 jit_solution(5623076393238082947)
XLA Ops:
  7.2 6.1 %reshape_squeeze.8 = bf16[1,16,57344]{2,0,1:T(2,128)(2,1)} reshape(bf16[1,1,3584,256]{3,2,1,0:T(8,128)(2,1)} %param.10) | data formatting | bytes 3670016 | tf_op jit(solution)/shard_map/reshape;squeeze | solution.py:67
  13.3 0.5 broadcast.20
  13.8 12.4 %reduce.1 = bf16[16,57344]{1,0:T(8,128)(2,1)S(1)} reduce(bf16[16,1,57344]{2,1,0:T(2,128)(2,1)} %bitcast.28, bf16[]{:T(256)} %broadcast.20), dimensions={1}, to_apply=%bitcast.23.reduce_sub_computation | reduce | bytes 3670018
  26.2 2.5 %reshape.34 = bf16[16,2,28672]{2,1,0:T(2,128)(2,1)} reshape(bf16[16,57344]{1,0:T(8,128)(2,1)S(1)} %reduce.1) | data formatting | bytes 3670016
  28.6 7.4 %all-to-all-start = ((bf16[16,2,28672]{2,1,0:T(2,128)(2,1)}), bf16[16,2,28672]{2,1,0:T(2,128)(2,1)S(1)}, u32[]{:S(2)}, u32[]{:S(2)}) async-start(bf16[16,2,28672]{2,1,0:T(2,128)(2,1)} %reshape.34), calls=%async_computation | async-start | bytes 3670016 | tf_op jit(solution)/shard_map/all_to_all | solution.py:70
  36.0 3.8 %copy.24 = bf16[1,1,256,3584]{2,3,1,0:T(8,128)(2,1)} copy(bf16[1,1,256,3584]{3,2,1,0:T(8,128)(2,1)} %param.11) | data formatting | bytes 3670016 | tf_op args[1]
  39.8 21.9 %all-to-all-done = bf16[16,2,28672]{2,1,0:T(2,128)(2,1)S(1)} async-done(((bf16[16,2,28672]{2,1,0:T(2,128)(2,1)}), bf16[16,2,28672]{2,1,0:T(2,128)(2,1)S(1)}, u32[]{:S(2)}, u32[]{:S(2)}) %all-to-all-start) | async-done | bytes 1835040 | tf_op jit(solution)/shard_map/all_to_all | solution.py:70
  61.8 0.0 copy-start
  61.8 1.2 copy-done
  63.0 5.1 %all-to-all-start.1 = ((bf16[256,16,224]{0,2,1:T(8,128)(2,1)}), bf16[256,16,224]{0,2,1:T(8,128)(2,1)S(1)}, u32[]{:S(2)}, u32[]{:S(2)}) async-start(bf16[256,16,224]{0,2,1:T(8,128)(2,1)} %bitcast), calls=%async_computation.1 | async-start | bytes 3670016 | tf_op jit(solution)/shard_map/all_to_all | solution.py:71
  68.1 0.0 all-gather.2.cloned.1.call-start
  68.2 10.2 %reshape.35 = bf16[16,1,57344]{2,1,0:T(2,128)(2,1)} reshape(bf16[16,2,28672]{2,1,0:T(2,128)(2,1)} %copy-done) | data formatting | bytes 3670016
  78.4 6.7 %convert_reduce_fusion.1 = f32[57344]{0:T(1024)S(1)} fusion(bf16[16,1,57344]{2,1,0:T(2,128)(2,1)} %reshape.35), kind=kLoop, calls=%fused_computation.1 | loop fusion | flops 1777664 | bytes 2064384 | tf_op jit(solution)/shard_map/reduce_sum | solution.py:73
  85.1 0.0 copy-start.1
  85.1 0.0 copy-start.5
  85.1 0.0 copy-start.6
  85.1 0.0 copy-start.7
  85.1 0.0 copy-start.8
  85.1 0.1 reshape.30
  85.2 6.4 %all-to-all-done.1 = bf16[256,16,224]{0,2,1:T(8,128)(2,1)S(1)} async-done(((bf16[256,16,224]{0,2,1:T(8,128)(2,1)}), bf16[256,16,224]{0,2,1:T(8,128)(2,1)S(1)}, u32[]{:S(2)}, u32[]{:S(2)}) %all-to-all-start.1) | async-done | bytes 1835040 | tf_op jit(solution)/shard_map/all_to_all | solution.py:71
  91.7 0.2 convert_reduce_fusion
  91.9 0.0 copy-done.1
  91.9 0.0 copy-start.2
  91.9 0.0 copy-start.3
  91.9 0.0 copy-start.4
  92.0 0.7 multiply_reduce_fusion
  92.6 0.0 copy-done.5
  92.6 0.7 multiply_reduce_fusion.1
  94.6 9.0 %psum.28 = f32[]{:T(128)} all-reduce(f32[]{:T(128)S(6)} %add.52), channel_id=1, replica_groups=mesh['dp_0'=4,'dp_1'=4,'mp_0'=8,'mp_1'=2] {'dp_0'}, use_global_device_ids=true, to_apply=%region_4.0 | all-reduce | flops 1 | bytes 8 | tf_op jit(solution)/shard_map/psum | solution.py:23
  103.6 9.8 %psum.29 = f32[]{:T(128)} all-reduce(f32[]{:T(128)} %psum.28), channel_id=1, replica_groups=mesh['dp_0'=4,'dp_1'=4,'mp_0'=8,'mp_1'=2] {'dp_1'}, use_global_device_ids=true, to_apply=%region_5.0 | all-reduce | flops 1 | bytes 8 | tf_op jit(solution)/shard_map/psum | solution.py:23
  113.4 20.6 %psum.30 = f32[]{:T(128)} all-reduce(f32[]{:T(128)} %psum.29), channel_id=1, replica_groups=mesh['dp_0'=4,'dp_1'=4,'mp_0'=8,'mp_1'=2] {'mp_0'}, use_global_device_ids=true, to_apply=%region_6.0 | all-reduce | flops 1 | bytes 8 | tf_op jit(solution)/shard_map/psum | solution.py:23
  134.0 3.1 %psum.31 = f32[]{:T(128)} all-reduce(f32[]{:T(128)} %psum.30), channel_id=1, replica_groups=mesh['dp_0'=4,'dp_1'=4,'mp_0'=8,'mp_1'=2] {'mp_1'}, use_global_device_ids=true, to_apply=%region_7.0 | all-reduce | flops 1 | bytes 8 | tf_op jit(solution)/shard_map/psum | solution.py:23
  137.8 0.0 copy-done.6
  137.8 0.0 copy-done.7
  137.8 0.0 copy-done.8
  137.8 1.0 convert_bitcast_fusion
  138.8 0.0 copy-done.2
  138.8 0.0 copy-done.3
  138.8 0.0 copy-done.4
  138.8 1.0 convert_bitcast_fusion.1
  139.7 0.7 pad_maximum_fusion
  140.4 0.0 all-gather.2.cloned.1.call-update
  140.4 48.7 %all-gather.2.cloned.1.call-done = bf16[3584,512]{1,0:T(8,128)(2,1)} async-done(((bf16[224,512]{1,0:T(8,128)(2,1)}), bf16[3584,512]{1,0:T(8,128)(2,1)}) %all-gather.2.cloned.1.call-update) | async-done | bytes 3670032 | tf_op jit(solution)/shard_map/all_gather | solution.py:31
  189.2 3.5 %slice_bitcast_fusion = (bf16[1,256,3584]{1,2,0:T(8,128)(2,1)S(1)}, bf16[1,3584,256]{2,1,0:T(8,128)(2,1)}) fusion(bf16[3584,512]{1,0:T(8,128)(2,1)} %all-gather.2.cloned.1.call-done), kind=kLoop, calls=%fused_computation.2 | loop fusion | bytes 7340032 | tf_op jit(solution)/shard_map/transpose | solution.py:35
  192.7 2.5 %copy.25 = bf16[1,256,3584]{2,1,0:T(8,128)(2,1)} copy(bf16[1,256,3584]{1,2,0:T(8,128)(2,1)S(1)} %get-tuple-element.50) | data formatting | bytes 3670016
Async XLA Ops:
  28.6 33.1 %all-to-all-start = ((bf16[16,2,28672]{2,1,0:T(2,128)(2,1)}), bf16[16,2,28672]{2,1,0:T(2,128)(2,1)S(1)}, u32[]{:S(2)}, u32[]{:S(2)}) async-start(bf16[16,2,28672]{2,1,0:T(2,128)(2,1)} %reshape.34), calls=%async_computation | async-start | bytes 3670016 | tf_op jit(solution)/shard_map/all_to_all | solution.py:70
  61.8 1.2 copy-start
  63.0 28.6 %all-to-all-start.1 = ((bf16[256,16,224]{0,2,1:T(8,128)(2,1)}), bf16[256,16,224]{0,2,1:T(8,128)(2,1)S(1)}, u32[]{:S(2)}, u32[]{:S(2)}) async-start(bf16[256,16,224]{0,2,1:T(8,128)(2,1)} %bitcast), calls=%async_computation.1 | async-start | bytes 3670016 | tf_op jit(solution)/shard_map/all_to_all | solution.py:71
  68.1 121.1 %all-gather.2.cloned.1.call-start = ((), (), s32[]{:S(2)}) async-start(), calls=%async_computation.2 | async-start | bytes 3899392 | tf_op jit(solution)/shard_map/all_gather | solution.py:31
  85.1 6.8 %copy-start.1 = (f32[1,256,224]{1,2,0:T(8,128)S(1)}, f32[1,256,224]{1,2,0:T(8,128)}, u32[]{:S(2)}) copy-start(f32[1,256,224]{1,2,0:T(8,128)} %param.13) | copy-start | bytes 688132
  85.1 7.5 %copy-start.5 = (f32[1,224,256]{2,1,0:T(8,128)S(1)}, f32[1,224,256]{2,1,0:T(8,128)}, u32[]{:S(2)}) copy-start(f32[1,224,256]{2,1,0:T(8,128)} %param.12) | copy-start | bytes 688132
  85.1 52.7 %copy-start.6 = (f32[1,256,224]{1,2,0:T(8,128)S(1)}, f32[1,256,224]{1,2,0:T(8,128)}, u32[]{:S(2)}) copy-start(f32[1,256,224]{1,2,0:T(8,128)} %param.15) | copy-start | bytes 688132
  85.1 52.7 %copy-start.7 = (f32[1,256,224]{1,2,0:T(8,128)S(1)}, f32[1,256,224]{1,2,0:T(8,128)}, u32[]{:S(2)}) copy-start(f32[1,256,224]{1,2,0:T(8,128)} %param.17) | copy-start | bytes 688132
  85.1 52.7 %copy-start.8 = (f32[1,256,224]{1,2,0:T(8,128)S(1)}, f32[1,256,224]{1,2,0:T(8,128)}, u32[]{:S(2)}) copy-start(f32[1,256,224]{1,2,0:T(8,128)} %param.19) | copy-start | bytes 688132
  91.9 46.8 %copy-start.2 = (f32[1,224,256]{2,1,0:T(8,128)S(1)}, f32[1,224,256]{2,1,0:T(8,128)}, u32[]{:S(2)}) copy-start(f32[1,224,256]{2,1,0:T(8,128)} %param.14) | copy-start | bytes 688132
  91.9 46.8 %copy-start.3 = (f32[1,224,256]{2,1,0:T(8,128)S(1)}, f32[1,224,256]{2,1,0:T(8,128)}, u32[]{:S(2)}) copy-start(f32[1,224,256]{2,1,0:T(8,128)} %param.16) | copy-start | bytes 688132
  91.9 46.8 %copy-start.4 = (f32[1,224,256]{2,1,0:T(8,128)S(1)}, f32[1,224,256]{2,1,0:T(8,128)}, u32[]{:S(2)}) copy-start(f32[1,224,256]{2,1,0:T(8,128)} %param.18) | copy-start | bytes 688132
Sparse Core Ops, SparseCore 0:
  140.6 48.5 all-gather.1
where the time goes:
time: 204 us; the launch traced here: 202 us
  waiting for transfers between devices  77.1 us (38%)
  blocking collectives  42.5 us (21%)
  local copies, waits for them, and re-layouts  30.5 us (15%)
  other arithmetic  23.3 us (11%)
  between operations  16.2 us (8%)
  starting transfers between devices  12.5 us (6%)
    all_gather x1, waiting for transfers between devices, turned_gather(): out = lax.all_gather(both, axis, axis=0, tiled=True)  48.7 us
    psum x4, blocking collectives, by_axis(): value = lax.psum(value, axis)  42.5 us
    all_to_all x1, waiting for transfers between devices, on_device(): lax.all_to_all(query_flat, DP, split_axis=1, concat_axis=1, tiled=True)  21.9 us
    unnamed x23, local copies, waits for them, and re-layouts  20.8 us
    unnamed x1, other arithmetic  12.4 us
    all_to_all x1, starting transfers between devices, on_device(): lax.all_to_all(query_flat, DP, split_axis=1, concat_axis=1, tiled=True)  7.39 us
    reduce_sum x1, other arithmetic, on_device(): jnp.sum(query_parts, axis=1, dtype=jnp.float32)  6.68 us
    all_to_all x1, waiting for transfers between devices, on_device(): lax.all_to_all(merge_flat, DP, split_axis=1, concat_axis=1, tiled=True)  6.44 us
  transfers between devices with their start and end apart: 3, of which 3 were waited for; matrix products, arithmetic and copies ran while one was open for 10% of the time, Pallas kernels for 0%

commit v1 on v0

v1 whole, which is shorter than its diff:
```python
import jax
import jax.numpy as jnp
from jax import lax
from jax.experimental import pallas as pl
from jax.experimental.pallas import tpu as pltpu
from jax.sharding import Mesh
from jax.sharding import PartitionSpec as P

STEP = 10
ENTRIES = 29360128
BETA_ONE = 0.9
BETA_TWO = 0.95
LEARN_RATE = 0.002
WEIGHT_DECAY = 0.1
ADAM_EPS = 1e-08

N = 4
ROWS = 224
COLS = 256
HALF = ROWS // 2
GROUP = N * ROWS
FULL = N * GROUP
BLOCK = 32
MESH_ID = pl.DeviceIdType.MESH
OFFSETS = (2, 1, 3, 0)

RELAY_A, RELAY_B, DIRECT_P, DIRECT_M, FORWARD_A, FORWARD_B = range(6)
T_A, T_B, U_P, U_M, V_P, V_M = range(6)


def wrap(value):
    return lax.rem(value, N)


def shard_rows(index, start=0, size=ROWS):
    return pl.ds(pl.multiple_of(index * ROWS + start, 16), size)


def kernel(
    grads_q, grads_m, accum_q, accum_m, master_q, master_m, moment_q, moment_m, second_q, second_m,
    weight_q, weight_m, shard_q, shard_m, first_q, first_m, variance_q, variance_m,
    raw_m, turned_m, own_q, held, relay, partial, t_buf, u_buf, v_buf, state, gather_m,
    plane_buf, column_buf, row_buf,
    load_sem, rs_send, rs_recv, second_send, second_recv, ag_send, ag_recv, ar_send, ar_recv,
):
    x, y = lax.axis_index("x"), lax.axis_index("y")
    z, c = lax.axis_index("z"), lax.axis_index("c")
    first_axis, second_axis = ("y", "x"), ("x", "y")
    f, s = (y, x), (x, y)

    def shard_index(a, fi, si):
        return si * N + fi if a == 0 else fi * N + si

    plane_peers, column_peers = [], []
    me_plane, me_column = x * N + y, z * 2 + c
    for d in range(1, 16):
        peer = lax.rem(me_plane + d, 16)
        plane_peers.append({"x": peer // N, "y": lax.rem(peer, N), "z": z, "c": c})
        peer = lax.rem(me_column + d, 16)
        column_peers.append({"x": x, "y": y, "z": peer // 2, "c": lax.rem(peer, 2)})

    def group_cols(fi):
        return pl.ds(pl.multiple_of(fi * GROUP, 128), GROUP)

    raw_loads = []
    for d in (2, 1, 3, 0):
        fi = wrap(x + d)
        copy = pltpu.make_async_copy(
            grads_m.at[:, group_cols(fi)], raw_m.at[:, group_cols(fi)], load_sem.at[d]
        )
        copy.start()
        raw_loads.append(copy)

    barrier = pltpu.get_barrier_semaphore()
    for peer in plane_peers + column_peers:
        pl.semaphore_signal(barrier, inc=1, device_id=peer, device_id_type=MESH_ID)

    own_loads = []
    for k in range(N):
        si = wrap(x + OFFSETS[k])
        copy = pltpu.make_async_copy(
            grads_q.at[shard_rows(si * N + y)], own_q.at[k], load_sem.at[4 + k]
        )
        copy.start()
        own_loads.append(copy)
    state_loads = []
    for i, ref in enumerate(
        (accum_q, accum_m, master_q, master_m, moment_q, moment_m, second_q, second_m)
    ):
        copy = pltpu.make_async_copy(ref, state.at[i], load_sem.at[8 + i])
        copy.start()
        state_loads.append(copy)

    pl.semaphore_wait(barrier, 30)

    def remote(src, dst, send, recv, axis, coordinate):
        return pltpu.make_async_remote_copy(
            src_ref=src,
            dst_ref=dst,
            send_sem=send,
            recv_sem=recv,
            device_id={axis: coordinate},
            device_id_type=MESH_ID,
        )

    started = []

    def go(copy):
        copy.start()
        started.append(copy)

    source = (grads_q, turned_m)

    def rs_copy(a, k, kind):
        fi, si = f[a], wrap(s[a] + OFFSETS[k])
        plus, minus, far = wrap(fi + 1), wrap(fi + 3), wrap(fi + 2)
        src = {
            RELAY_A: lambda: source[a].at[shard_rows(shard_index(a, far, si), 0, HALF)],
            RELAY_B: lambda: source[a].at[shard_rows(shard_index(a, far, si), HALF, HALF)],
            DIRECT_P: lambda: source[a].at[shard_rows(shard_index(a, plus, si))],
            DIRECT_M: lambda: source[a].at[shard_rows(shard_index(a, minus, si))],
            FORWARD_A: lambda: relay.at[a, k, 0],
            FORWARD_B: lambda: relay.at[a, k, 1],
        }[kind]()
        dst = {
            RELAY_A: lambda: relay.at[a, k, 0],
            RELAY_B: lambda: relay.at[a, k, 1],
            DIRECT_P: lambda: held.at[a, k, 0],
            DIRECT_M: lambda: held.at[a, k, 1],
            FORWARD_A: lambda: held.at[a, k, 2, pl.ds(0, HALF)],
            FORWARD_B: lambda: held.at[a, k, 2, pl.ds(HALF, HALF)],
        }[kind]()
        target = plus if kind in (RELAY_A, DIRECT_P, FORWARD_A) else minus
        return remote(
            src, dst, rs_send.at[a, k, kind], rs_recv.at[a, k, kind], first_axis[a], target
        )

    def raw_relay(a, k):
        go(rs_copy(a, k, RELAY_A))
        go(rs_copy(a, k, RELAY_B))

    def raw_direct(a, k):
        go(rs_copy(a, k, DIRECT_P))
        go(rs_copy(a, k, DIRECT_M))

    def forward(a, k):
        rs_copy(a, k, RELAY_A).wait_recv()
        go(rs_copy(a, k, FORWARD_A))
        rs_copy(a, k, RELAY_B).wait_recv()
        go(rs_copy(a, k, FORWARD_B))

    def turn(fi):
        def step(i, carry):
            at = pl.ds(pl.multiple_of(fi * GROUP + i * 128, 128), 128)
            turned_m[at, :] = raw_m[:, at].T
            return carry

        lax.fori_loop(0, GROUP // 128, step, 0)

    def add_up(a, k):
        for kind in (DIRECT_P, DIRECT_M, FORWARD_A, FORWARD_B):
            rs_copy(a, k, kind).wait_recv()
        if a == 0:
            own_loads[k].wait()
        if k == 3:
            state_loads[a].wait()
        own_base = 0 if a == 0 else shard_index(a, f[a], wrap(s[a] + OFFSETS[k])) * ROWS

        def step(i, carry):
            at = pl.ds(pl.multiple_of(i * BLOCK, BLOCK), BLOCK)
            if a == 0:
                mine = own_q[k, at, :]
            else:
                mine = turned_m[pl.ds(pl.multiple_of(own_base + i * BLOCK, BLOCK), BLOCK), :]
            value = mine.astype(jnp.float32)
            for j in range(3):
                value = value + held[a, k, j, at, :].astype(jnp.float32)
            if k == 3:
                value = value + state[a, at, :]
            partial[a, k, at, :] = value
            return carry

        lax.fori_loop(0, ROWS // BLOCK, step, 0)

    low, high = pl.ds(0, HALF), pl.ds(HALF, HALF)

    def second_copy(a, kind):
        plus, minus = wrap(s[a] + 1), wrap(s[a] + 3)
        src, dst, target = {
            T_A: (partial.at[a, 0, low], t_buf.at[a, 0], plus),
            T_B: (partial.at[a, 0, high], t_buf.at[a, 1], minus),
            U_P: (partial.at[a, 1, high], u_buf.at[a, 0], plus),
            U_M: (partial.at[a, 2, low], u_buf.at[a, 1], minus),
            V_P: (partial.at[a, 1, low], v_buf.at[a, 0], plus),
            V_M: (partial.at[a, 2, high], v_buf.at[a, 1], minus),
        }[kind]
        return remote(
            src, dst, second_send.at[a, kind], second_recv.at[a, kind], second_axis[a], target
        )

    def merge_t(a):
        second_copy(a, T_A).wait_recv()
        partial[a, 1, 0:HALF, :] = partial[a, 1, 0:HALF, :] + t_buf[a, 0]
        go(second_copy(a, V_P))
        second_copy(a, T_B).wait_recv()
        partial[a, 2, HALF:ROWS, :] = partial[a, 2, HALF:ROWS, :] + t_buf[a, 1]
        go(second_copy(a, V_M))

    def squares(value):
        return jnp.sum((value * value).reshape(-1, 8, COLS), axis=0)

    def finish(a, acc):
        for kind in (U_P, U_M, V_P, V_M):
            second_copy(a, kind).wait_recv()
        for h, one, two in ((0, v_buf, u_buf), (1, u_buf, v_buf)):
            def step(i, acc):
                at = pl.ds(pl.multiple_of(i * 16, 16), 16)
                here = pl.ds(pl.multiple_of(h * HALF + i * 16, 16), 16)
                total = partial[a, 3, here, :] + one[a, 0, at, :] + two[a, 1, at, :]
                partial[a, 3, here, :] = total
                return acc + squares(total)

            acc = lax.fori_loop(0, HALF // 16, step, acc)
        return acc

    raw_relay(0, 0)
    raw_direct(0, 0)
    raw_relay(0, 1)
    raw_direct(0, 1)
    raw_loads[0].wait()
    turn(wrap(x + 2))
    raw_relay(1, 0)
    raw_loads[1].wait()
    turn(wrap(x + 1))
    go(rs_copy(1, 0, DIRECT_P))
    raw_loads[2].wait()
    turn(wrap(x + 3))
    go(rs_copy(1, 0, DIRECT_M))
    raw_relay(1, 1)
    raw_direct(1, 1)
    raw_loads[3].wait()
    turn(x)
    for k in (0, 1):
        for a in (0, 1):
            forward(a, k)
            raw_relay(a, k + 2)
            raw_direct(a, k + 2)
    for a in (0, 1):
        forward(a, 2)
        add_up(a, 0)
        go(second_copy(a, T_A))
        go(second_copy(a, T_B))
    for a in (0, 1):
        forward(a, 3)
        add_up(a, 1)
        go(second_copy(a, U_P))
    for a in (0, 1):
        add_up(a, 2)
        go(second_copy(a, U_M))
    for a in (0, 1):
        merge_t(a)
    for a in (0, 1):
        add_up(a, 3)
    acc = jnp.zeros((8, COLS), jnp.float32)
    for a in (0, 1):
        acc = finish(a, acc)

    def exchange(stage, row, buf, me, peers):
        row_buf[stage] = row
        buf[me] = row
        for d, peer in enumerate(peers):
            copy = pltpu.make_async_remote_copy(
                src_ref=row_buf.at[stage],
                dst_ref=buf.at[me],
                send_sem=ar_send.at[stage, d],
                recv_sem=ar_recv.at[stage, d],
                device_id=peer,
                device_id_type=MESH_ID,
            )
            go(copy)
        for d in range(15):
            sender = lax.rem(me + 15 - d, 16)
            pltpu.make_async_remote_copy(
                src_ref=row_buf.at[stage],
                dst_ref=buf.at[sender],
                send_sem=ar_send.at[stage, d],
                recv_sem=ar_recv.at[stage, d],
                device_id=peers[d],
                device_id_type=MESH_ID,
            ).wait_recv()
        return jnp.sum(buf[...], axis=0)

    row = jnp.sum(acc, axis=0, keepdims=True)
    row = row[:, :128] + row[:, 128:]
    row = exchange(0, row, plane_buf, me_plane, plane_peers)
    row = exchange(1, row, column_buf, me_column, column_peers)
    sumsq = jnp.sum(row, axis=1, keepdims=True)
    clip = jnp.minimum(1.0, lax.rsqrt(sumsq / float(ENTRIES) + 1e-06))

    gathered = (weight_q, gather_m)
    outs = ((shard_q, first_q, variance_q), (shard_m, first_m, variance_m))
    for copy in state_loads[2:]:
        copy.wait()

    def update(a):
        base = shard_index(a, f[a], s[a]) * ROWS
        shard_out, first_out, variance_out = outs[a]

        def step(i, carry):
            at = pl.ds(pl.multiple_of(i * BLOCK, BLOCK), BLOCK)
            scaled = clip * partial[a, 3, at, :]
            master = state[2 + a, at, :]
            first = BETA_ONE * state[4 + a, at, :] + (1.0 - BETA_ONE) * scaled
            variance = BETA_TWO * state[6 + a, at, :] + (1.0 - BETA_TWO) * scaled * scaled
            corr_one = 1.0 - BETA_ONE**STEP
            corr_two = 1.0 - BETA_TWO**STEP
            change = (
                first / corr_one / (jnp.sqrt(variance / corr_two) + ADAM_EPS)
                + WEIGHT_DECAY * master
            )
            shard = master - LEARN_RATE * change
            shard_out[at, :] = shard
            first_out[at, :] = first
            variance_out[at, :] = variance
            gathered[a][pl.ds(pl.multiple_of(base + i * BLOCK, BLOCK), BLOCK), :] = shard.astype(
                jnp.bfloat16
            )
            return carry

        lax.fori_loop(0, ROWS // BLOCK, step, 0)

    ITEMS = (0, 3, 1, 2)

    def ag_copy(a, item, kind):
        if item == 0:
            axis, here = second_axis[a], s[a]
        else:
            axis, here = first_axis[a], f[a]
        owner = {0: here, 1: here, 2: wrap(here + 3), 3: wrap(here + 1)}[kind]
        if item == 0:
            index = shard_index(a, f[a], owner)
        else:
            index = shard_index(a, owner, wrap(s[a] + ITEMS[item - 1]))
        start, size = {0: (0, ROWS), 1: (0, ROWS), 2: (0, HALF), 3: (HALF, HALF)}[kind]
        ref = gathered[a].at[shard_rows(index, start, size)]
        target = wrap(here + 1) if kind in (0, 2) else wrap(here + 3)
        return remote(ref, ref, ag_send.at[a, item, kind], ag_recv.at[a, item, kind], axis, target)

    def ag_wait(a, item, kind):
        if item == 0:
            axis, here = second_axis[a], s[a]
        else:
            axis, here = first_axis[a], f[a]
        owner = {0: wrap(here + 3), 1: wrap(here + 1), 2: wrap(here + 2), 3: wrap(here + 2)}[kind]
        if item == 0:
            index = shard_index(a, f[a], owner)
        else:
            index = shard_index(a, owner, wrap(s[a] + ITEMS[item - 1]))
        start, size = {0: (0, ROWS), 1: (0, ROWS), 2: (0, HALF), 3: (HALF, HALF)}[kind]
        ref = gathered[a].at[shard_rows(index, start, size)]
        remote(
            ref, ref, ag_send.at[a, item, kind], ag_recv.at[a, item, kind], axis, here
        ).wait_recv()

    def turn_back(fi):
        def step(i, carry):
            at = pl.ds(pl.multiple_of(fi * GROUP + i * 128, 128), 128)
            weight_m[:, at] = gather_m[at, :].T
            return carry

        lax.fori_loop(0, GROUP // 128, step, 0)

    for a in (0, 1):
        update(a)
        for item in (0, 1):
            go(ag_copy(a, item, 0))
            go(ag_copy(a, item, 1))
    for a in (0, 1):
        ag_wait(a, 0, 0)
        go(ag_copy(a, 0, 2))
        ag_wait(a, 0, 1)
        go(ag_copy(a, 0, 3))
        for item in (2, 3):
            go(ag_copy(a, item, 0))
            go(ag_copy(a, item, 1))

    def ag_forward(a, item):
        ag_wait(a, item, 0)
        go(ag_copy(a, item, 2))
        ag_wait(a, item, 1)
        go(ag_copy(a, item, 3))

    for a in (0, 1):
        ag_forward(a, 1)
    for a in (0, 1):
        ag_wait(a, 0, 2)
        ag_wait(a, 0, 3)
        go(ag_copy(a, 4, 0))
        go(ag_copy(a, 4, 1))
    turn_back(x)
    for item in (2, 3, 4):
        for a in (0, 1):
            ag_forward(a, item)
    turn_back(wrap(x + 1))
    turn_back(wrap(x + 3))
    for item in (1, 2, 3, 4):
        for a in (0, 1):
            ag_wait(a, item, 2)
            ag_wait(a, item, 3)
    turn_back(wrap(x + 2))
    for copy in started:
        copy.wait_send()


def on_device(
    query_grads, merge_grads, query_accum, merge_accum, query_master, merge_master,
    query_moment, merge_moment, query_second, merge_second,
):
    def flat(value):
        return value.reshape(ROWS, COLS)

    def turned(value):
        return jnp.swapaxes(value[0], 0, 1)

    bf16, f32 = jnp.bfloat16, jnp.float32
    any_spec = pl.BlockSpec(memory_space=pl.ANY)
    shard = pltpu.VMEM((ROWS, COLS), f32)
    outs = pl.pallas_call(
        kernel,
        name="adamw_step",
        out_shape=[
            pltpu.VMEM((FULL, COLS), bf16),
            pltpu.VMEM((COLS, FULL), bf16),
            shard, shard, shard, shard, shard, shard,
        ],
        in_specs=[any_spec] * 10,
        out_specs=[pl.BlockSpec(memory_space=pltpu.VMEM)] * 8,
        scratch_shapes=[
            pltpu.VMEM((COLS, FULL), bf16),
            pltpu.VMEM((FULL, COLS), bf16),
            pltpu.VMEM((N, ROWS, COLS), bf16),
            pltpu.VMEM((2, N, 3, ROWS, COLS), bf16),
            pltpu.VMEM((2, N, 2, HALF, COLS), bf16),
            pltpu.VMEM((2, N, ROWS, COLS), f32),
            pltpu.VMEM((2, 2, HALF, COLS), f32),
            pltpu.VMEM((2, 2, HALF, COLS), f32),
            pltpu.VMEM((2, 2, HALF, COLS), f32),
            pltpu.VMEM((8, ROWS, COLS), f32),
            pltpu.VMEM((FULL, COLS), bf16),
            pltpu.VMEM((16, 1, 128), f32),
            pltpu.VMEM((16, 1, 128), f32),
            pltpu.VMEM((2, 1, 128), f32),
            pltpu.SemaphoreType.DMA((16,)),
            pltpu.SemaphoreType.DMA((2, N, 6)),
            pltpu.SemaphoreType.DMA((2, N, 6)),
            pltpu.SemaphoreType.DMA((2, 6)),
            pltpu.SemaphoreType.DMA((2, 6)),
            pltpu.SemaphoreType.DMA((2, 5, 4)),
            pltpu.SemaphoreType.DMA((2, 5, 4)),
            pltpu.SemaphoreType.DMA((2, 15)),
            pltpu.SemaphoreType.DMA((2, 15)),
        ],
        compiler_params=pltpu.CompilerParams(
            collective_id=0, has_side_effects=True, vmem_limit_bytes=32 * 2**20
        ),
    )(
        query_grads.reshape(FULL, COLS), merge_grads.reshape(COLS, FULL),
        flat(query_accum), turned(merge_accum), flat(query_master), turned(merge_master),
        flat(query_moment), turned(merge_moment), flat(query_second), turned(merge_second),
    )
    weight_q, weight_m, shard_q, shard_m, first_q, first_m, variance_q, variance_m = outs

    def back(value):
        return jnp.swapaxes(value, 0, 1)[None]

    return (
        weight_q[None], weight_m[None],
        shard_q[None], back(shard_m), first_q[None], back(first_m), variance_q[None], back(variance_m),
    )


def solution(mesh):
    finer = Mesh(mesh.devices.reshape(4, 4, 8, 2), ("x", "y", "z", "c"))
    dp, mp = ("x", "y"), ("z", "c")
    query, merge = P(None, dp, mp), P(None, mp, dp)
    return jax.shard_map(
        on_device,
        mesh=finer,
        in_specs=(P(dp, None, None, mp), P(dp, None, mp, None)) + (query, merge) * 4,
        out_specs=(P(None, None, mp), P(None, mp, None)) + (query, merge) * 3,
        check_vma=False,
    )
```

time: 204 us -> 94.2 us (0.46)
  waiting for transfers between devices: 77.1 us -> 0 us
  Pallas kernels: 0 us -> 75.3 us
  blocking collectives: 42.5 us -> 0 us
  other arithmetic: 23.3 us -> 0 us
  between operations: 16.2 us -> 0.67 us
  local copies, waits for them, and re-layouts: 30.5 us -> 17.1 us
  starting transfers between devices: 12.5 us -> 0 us
    pallas_call x0 -> x1, Pallas kernels: none -> 75.3 us  [on_device(): pl.pallas_call(kernel, name='adamw_step', out_shape=[pltpu.VMEM((FULL, CO...]
    all_gather x1 -> x0, waiting for transfers between devices: 48.7 us -> none  [turned_gather(): out = lax.all_gather(both, axis, axis=0, tiled=True)]
    psum x4 -> x0, blocking collectives: 42.5 us -> none  [by_axis(): value = lax.psum(value, axis)]
    all_to_all x2 -> x0, waiting for transfers between devices: 28.4 us -> none  [the longest x1 21.9 us: on_device(): lax.all_to_all(query_flat, DP, split_axis=1, concat_axis=1, tiled=True)]
    all_to_all x2 -> x0, starting transfers between devices: 12.5 us -> none  [the longest x1 7.39 us: on_device(): lax.all_to_all(query_flat, DP, split_axis=1, concat_axis=1, tiled=True)]
    unnamed x1 -> x0, other arithmetic: 12.4 us -> none
    reduce_sum x4 -> x0, other arithmetic: 8.25 us -> none  [the longest x1 6.68 us: on_device(): jnp.sum(query_parts, axis=1, dtype=jnp.float32)]
    another operation x1 -> x0, local copies, waits for them, and re-layouts: 6.13 us -> none  [on_device(): query_grads[0].reshape(layers, owners, width // owners * heads_local)]
  transfers between devices with their start and end apart: 3 -> 0, of which waited for: 3 -> 0; matrix products, arithmetic and copies ran while one was open for 10% -> 0% of each run, Pallas kernels for 0% -> 0%
where the time goes in v1:
time: 94.2 us; the launch traced here: 93 us
  Pallas kernels  75.3 us (80%)
  local copies, waits for them, and re-layouts  17.1 us (18%)
    pallas_call x1, Pallas kernels, on_device(): pl.pallas_call(kernel, name='adamw_step', out_shape=[pltpu.VMEM((FULL, CO...  75.3 us
    unnamed x28, local copies, waits for them, and re-layouts  17.1 us

profile of v1, /device:TPU:8, one launch (start us, length us, event | category | flops | bytes accessed | tf_op | source)
XLA Modules:
  0.0 93.0 jit_solution(17883016942639648401)
XLA Ops:
  0.6 0.0 copy-start
  0.6 1.5 %copy-done = bf16[1,1,3584,256]{3,2,1,0:T(8,128)(2,1)S(1)} copy-done((bf16[1,1,3584,256]{3,2,1,0:T(8,128)(2,1)S(1)}, bf16[1,1,3584,256]{3,2,1,0:T(8,128)(2,1)}, u32[]{:S(2)}) %copy-start) | copy-done | bytes 1835032
  2.1 0.0 copy-start.1
  2.1 1.5 %copy-done.1 = bf16[1,1,256,3584]{3,2,1,0:T(8,128)(2,1)S(1)} copy-done((bf16[1,1,256,3584]{3,2,1,0:T(8,128)(2,1)S(1)}, bf16[1,1,256,3584]{3,2,1,0:T(8,128)(2,1)}, u32[]{:S(2)}) %copy-start.1) | copy-done | bytes 1835032
  3.6 0.0 copy-start.2
  3.6 0.9 %copy-done.2 = f32[1,224,256]{2,1,0:T(8,128)S(1)} copy-done((f32[1,224,256]{2,1,0:T(8,128)S(1)}, f32[1,224,256]{2,1,0:T(8,128)}, u32[]{:S(2)}) %copy-start.2) | copy-done | bytes 229400
  4.6 0.0 copy-start.3
  4.6 0.9 %copy-done.3 = f32[1,256,224]{1,2,0:T(8,128)S(1)} copy-done((f32[1,256,224]{1,2,0:T(8,128)S(1)}, f32[1,256,224]{1,2,0:T(8,128)}, u32[]{:S(2)}) %copy-start.3) | copy-done | bytes 229400
  5.5 0.0 copy-start.4
  5.5 0.9 %copy-done.4 = f32[1,224,256]{2,1,0:T(8,128)S(1)} copy-done((f32[1,224,256]{2,1,0:T(8,128)S(1)}, f32[1,224,256]{2,1,0:T(8,128)}, u32[]{:S(2)}) %copy-start.4) | copy-done | bytes 229400
  6.5 0.0 copy-start.5
  6.5 0.9 %copy-done.5 = f32[1,256,224]{1,2,0:T(8,128)S(1)} copy-done((f32[1,256,224]{1,2,0:T(8,128)S(1)}, f32[1,256,224]{1,2,0:T(8,128)}, u32[]{:S(2)}) %copy-start.5) | copy-done | bytes 229400
  7.4 0.0 copy-start.6
  7.4 0.9 %copy-done.6 = f32[1,224,256]{2,1,0:T(8,128)S(1)} copy-done((f32[1,224,256]{2,1,0:T(8,128)S(1)}, f32[1,224,256]{2,1,0:T(8,128)}, u32[]{:S(2)}) %copy-start.6) | copy-done | bytes 229400
  8.3 0.0 copy-start.7
  8.3 0.9 %copy-done.7 = f32[1,256,224]{1,2,0:T(8,128)S(1)} copy-done((f32[1,256,224]{1,2,0:T(8,128)S(1)}, f32[1,256,224]{1,2,0:T(8,128)}, u32[]{:S(2)}) %copy-start.7) | copy-done | bytes 229400
  9.3 0.0 copy-start.8
  9.3 0.9 %copy-done.8 = f32[1,224,256]{2,1,0:T(8,128)S(1)} copy-done((f32[1,224,256]{2,1,0:T(8,128)S(1)}, f32[1,224,256]{2,1,0:T(8,128)}, u32[]{:S(2)}) %copy-start.8) | copy-done | bytes 229400
  10.2 0.0 copy-start.9
  10.2 0.9 %copy-done.9 = f32[1,256,224]{1,2,0:T(8,128)S(1)} copy-done((f32[1,256,224]{1,2,0:T(8,128)S(1)}, f32[1,256,224]{1,2,0:T(8,128)}, u32[]{:S(2)}) %copy-start.9) | copy-done | bytes 229400
  11.1 75.3 %adamw_step.1 = (bf16[3584,256]{1,0:T(8,128)(2,1)S(1)}, bf16[256,3584]{1,0:T(8,128)(2,1)S(1)}, f32[224,256]{1,0:T(8,128)S(1)}, f32[224,256]{1,0:T(8,128)S(1)}, f...) custom-call(bf16[3584,256]{1,0:T(8,128)(2,1)S(1)} %bitcast.40, ...), custom_call_target="tpu_custom_call" | custom-call | tf_op jit(solution)/shard_map/adamw_step/pallas_call | solution.py:428
  86.4 1.2 %copy.26 = bf16[1,3584,256]{2,1,0:T(8,128)(2,1)} copy(bf16[1,3584,256]{2,1,0:T(8,128)(2,1)S(1)} %bitcast.33) | data formatting | bytes 3670016
  87.7 1.2 %copy.27 = bf16[1,256,3584]{2,1,0:T(8,128)(2,1)} copy(bf16[1,256,3584]{2,1,0:T(8,128)(2,1)S(1)} %bitcast.32) | data formatting | bytes 3670016
  88.9 0.7 copy.28
  89.6 0.7 copy.29
  90.3 0.7 copy.30
  91.0 0.7 copy.31
  91.7 0.7 copy.32
  92.3 0.7 copy.33
Async XLA Ops:
  0.6 1.5 %copy-start = (bf16[1,1,3584,256]{3,2,1,0:T(8,128)(2,1)S(1)}, bf16[1,1,3584,256]{3,2,1,0:T(8,128)(2,1)}, u32[]{:S(2)}) copy-start(bf16[1,1,3584,256]{3,2,1,0:T(8,128)(2,1)} %param.10) | copy-start | bytes 5505028
  2.1 1.5 %copy-start.1 = (bf16[1,1,256,3584]{3,2,1,0:T(8,128)(2,1)S(1)}, bf16[1,1,256,3584]{3,2,1,0:T(8,128)(2,1)}, u32[]{:S(2)}) copy-start(bf16[1,1,256,3584]{3,2,1,0:T(8,128)(2,1)} %param.11) | copy-start | bytes 5505028
  3.6 0.9 %copy-start.2 = (f32[1,224,256]{2,1,0:T(8,128)S(1)}, f32[1,224,256]{2,1,0:T(8,128)}, u32[]{:S(2)}) copy-start(f32[1,224,256]{2,1,0:T(8,128)} %param.12) | copy-start | bytes 688132
  4.6 0.9 %copy-start.3 = (f32[1,256,224]{1,2,0:T(8,128)S(1)}, f32[1,256,224]{1,2,0:T(8,128)}, u32[]{:S(2)}) copy-start(f32[1,256,224]{1,2,0:T(8,128)} %param.13) | copy-start | bytes 688132
  5.5 0.9 %copy-start.4 = (f32[1,224,256]{2,1,0:T(8,128)S(1)}, f32[1,224,256]{2,1,0:T(8,128)}, u32[]{:S(2)}) copy-start(f32[1,224,256]{2,1,0:T(8,128)} %param.14) | copy-start | bytes 688132
  6.5 0.9 %copy-start.5 = (f32[1,256,224]{1,2,0:T(8,128)S(1)}, f32[1,256,224]{1,2,0:T(8,128)}, u32[]{:S(2)}) copy-start(f32[1,256,224]{1,2,0:T(8,128)} %param.15) | copy-start | bytes 688132
  7.4 0.9 %copy-start.6 = (f32[1,224,256]{2,1,0:T(8,128)S(1)}, f32[1,224,256]{2,1,0:T(8,128)}, u32[]{:S(2)}) copy-start(f32[1,224,256]{2,1,0:T(8,128)} %param.16) | copy-start | bytes 688132
  8.3 0.9 %copy-start.7 = (f32[1,256,224]{1,2,0:T(8,128)S(1)}, f32[1,256,224]{1,2,0:T(8,128)}, u32[]{:S(2)}) copy-start(f32[1,256,224]{1,2,0:T(8,128)} %param.17) | copy-start | bytes 688132
  9.3 0.9 %copy-start.8 = (f32[1,224,256]{2,1,0:T(8,128)S(1)}, f32[1,224,256]{2,1,0:T(8,128)}, u32[]{:S(2)}) copy-start(f32[1,224,256]{2,1,0:T(8,128)} %param.18) | copy-start | bytes 688132
  10.2 0.9 %copy-start.9 = (f32[1,256,224]{1,2,0:T(8,128)S(1)}, f32[1,256,224]{1,2,0:T(8,128)}, u32[]{:S(2)}) copy-start(f32[1,256,224]{1,2,0:T(8,128)} %param.19) | copy-start | bytes 688132

commit v2 on v1

--- a/solution.py
+++ b/solution.py
@@ -412,6 +412,18 @@
         copy.wait_send()
 
 
+def write_out(*refs):
+    sources, targets, sem = refs[:8], refs[8:16], refs[16]
+    copies = [
+        pltpu.make_async_copy(source, target, sem.at[i])
+        for i, (source, target) in enumerate(zip(sources, targets))
+    ]
+    for copy in copies:
+        copy.start()
+    for copy in copies:
+        copy.wait()
+
+
 def on_device(
     query_grads, merge_grads, query_accum, merge_accum, query_master, merge_master,
     query_moment, merge_moment, query_second, merge_second,
@@ -423,8 +435,14 @@
         return jnp.swapaxes(value[0], 0, 1)
 
     bf16, f32 = jnp.bfloat16, jnp.float32
-    any_spec = pl.BlockSpec(memory_space=pl.ANY)
+    hbm_spec = pl.BlockSpec(memory_space=pltpu.HBM)
     shard = pltpu.VMEM((ROWS, COLS), f32)
+    operands = (
+        query_grads.reshape(FULL, COLS), merge_grads.reshape(COLS, FULL),
+        flat(query_accum), turned(merge_accum), flat(query_master), turned(merge_master),
+        flat(query_moment), turned(merge_moment), flat(query_second), turned(merge_second),
+    )
+    operands = [pltpu.with_memory_space_constraint(value, pltpu.HBM) for value in operands]
     outs = pl.pallas_call(
         kernel,
         name="adamw_step",
@@ -433,7 +451,7 @@
             pltpu.VMEM((COLS, FULL), bf16),
             shard, shard, shard, shard, shard, shard,
         ],
-        in_specs=[any_spec] * 10,
+        in_specs=[hbm_spec] * 10,
         out_specs=[pl.BlockSpec(memory_space=pltpu.VMEM)] * 8,
         scratch_shapes=[
             pltpu.VMEM((COLS, FULL), bf16),
@@ -463,11 +481,16 @@
         compiler_params=pltpu.CompilerParams(
             collective_id=0, has_side_effects=True, vmem_limit_bytes=32 * 2**20
         ),
-    )(
-        query_grads.reshape(FULL, COLS), merge_grads.reshape(COLS, FULL),
-        flat(query_accum), turned(merge_accum), flat(query_master), turned(merge_master),
-        flat(query_moment), turned(merge_moment), flat(query_second), turned(merge_second),
-    )
+    )(*operands)
+    outs = pl.pallas_call(
+        write_out,
+        name="write_out",
+        out_shape=[jax.ShapeDtypeStruct(out.shape, out.dtype) for out in outs],
+        in_specs=[pl.BlockSpec(memory_space=pltpu.VMEM)] * 8,
+        out_specs=[hbm_spec] * 8,
+        scratch_shapes=[pltpu.SemaphoreType.DMA((8,))],
+        compiler_params=pltpu.CompilerParams(vmem_limit_bytes=2**20),
+    )(*outs)
     weight_q, weight_m, shard_q, shard_m, first_q, first_m, variance_q, variance_m = outs
 
     def back(value):

time: 94.2 us -> 78.7 us (0.84)
  local copies, waits for them, and re-layouts: 17.1 us -> 0 us
  Pallas kernels: 75.3 us -> 76.9 us
    unnamed x28 -> x0, local copies, waits for them, and re-layouts: 17.1 us -> none
    pallas_call x0 -> x1, Pallas kernels: none -> 2.33 us  [on_device(): pl.pallas_call(write_out, name='write_out', out_shape=[jax.ShapeDtypeStru...]
where the time goes in v2:
time: 78.7 us; the launch traced here: 77.5 us
  Pallas kernels  76.9 us (98%)
    pallas_call x1, Pallas kernels, on_device(): pl.pallas_call(kernel, name='adamw_step', out_shape=[pltpu.VMEM((FULL, CO...  74.5 us
    pallas_call x1, Pallas kernels, on_device(): pl.pallas_call(write_out, name='write_out', out_shape=[jax.ShapeDtypeStru...  2.33 us

profile of v2, /device:TPU:8, one launch (start us, length us, event | category | flops | bytes accessed | tf_op | source)
XLA Modules:
  0.0 77.5 jit_solution(17694832073974799093)
XLA Ops:
  0.6 74.5 %adamw_step.1 = (bf16[3584,256]{1,0:T(8,128)(2,1)S(1)}, bf16[256,3584]{1,0:T(8,128)(2,1)S(1)}, f32[224,256]{1,0:T(8,128)S(1)}, f32[224,256]{1,0:T(8,128)S(1)}, f...) custom-call(bf16[3584,256]{1,0:T(8,128)(2,1)} %bitcast.32, ...), custom_call_target="tpu_custom_call" | custom-call | tf_op jit(solution)/shard_map/adamw_step/pallas_call | solution.py:446
  75.2 2.3 %write_out.1 = (bf16[3584,256]{1,0:T(8,128)(2,1)}, bf16[256,3584]{1,0:T(8,128)(2,1)}, f32[224,256]{1,0:T(8,128)}, f32[224,256]{1,0:T(8,128)}, f32[224,256]{1,0:T...) custom-call(bf16[3584,256]{1,0:T(8,128)(2,1)S(1)} %get-tuple-element.24.refs_0_, ...), custom_call_target="tpu_custom_call" | custom-call | tf_op jit(solution)/shard_map/write_out/pallas_call | solution.py:485

commit v3 on v2

--- a/solution.py
+++ b/solution.py
@@ -24,7 +24,7 @@
 MESH_ID = pl.DeviceIdType.MESH
 OFFSETS = (2, 1, 3, 0)
 
-RELAY_A, RELAY_B, DIRECT_P, DIRECT_M, FORWARD_A, FORWARD_B = range(6)
+RELAY_A, RELAY_B, RAW_P, RAW_M, SUM_P, SUM_M = range(6)
 T_A, T_B, U_P, U_M, V_P, V_M = range(6)
 
 
@@ -39,9 +39,9 @@
 def kernel(
     grads_q, grads_m, accum_q, accum_m, master_q, master_m, moment_q, moment_m, second_q, second_m,
     weight_q, weight_m, shard_q, shard_m, first_q, first_m, variance_q, variance_m,
-    raw_m, turned_m, own_q, held, relay, partial, t_buf, u_buf, v_buf, state, gather_m,
+    raw_m, turned_m, raw_q, relay, raw_in, sum_in, sum_out, partial, send_s, t_buf, u_buf, v_buf, state, gather_m,
     plane_buf, column_buf, row_buf,
-    load_sem, rs_send, rs_recv, second_send, second_recv, ag_send, ag_recv, ar_send, ar_recv,
+    load_sem, rs_send, rs_recv, second_send, second_recv, ag_send, ag_recv, ar_send, ar_recv, hand,
 ):
     x, y = lax.axis_index("x"), lax.axis_index("y")
     z, c = lax.axis_index("z"), lax.axis_index("c")
@@ -72,17 +72,22 @@
         raw_loads.append(copy)
 
     barrier = pltpu.get_barrier_semaphore()
-    for peer in plane_peers + column_peers:
+    near_z = ({"z": lax.rem(z + 1, 8)}, {"z": lax.rem(z + 7, 8)})
+    for peer in (
+        {"x": wrap(x + 1)}, {"x": wrap(x + 3)}, {"y": wrap(y + 1)}, {"y": wrap(y + 3)}, *near_z
+    ):
         pl.semaphore_signal(barrier, inc=1, device_id=peer, device_id_type=MESH_ID)
 
-    own_loads = []
+    @pl.when(c == 0)
+    def _():
+        pl.semaphore_signal(barrier, inc=1, device_id={"c": 1}, device_id_type=MESH_ID)
+
+    query_loads = []
     for k in range(N):
-        si = wrap(x + OFFSETS[k])
-        copy = pltpu.make_async_copy(
-            grads_q.at[shard_rows(si * N + y)], own_q.at[k], load_sem.at[4 + k]
-        )
+        rows = pl.ds(pl.multiple_of(wrap(x + OFFSETS[k]) * GROUP, GROUP), GROUP)
+        copy = pltpu.make_async_copy(grads_q.at[rows], raw_q.at[rows], load_sem.at[4 + k])
         copy.start()
-        own_loads.append(copy)
+        query_loads.append(copy)
     state_loads = []
     for i, ref in enumerate(
         (accum_q, accum_m, master_q, master_m, moment_q, moment_m, second_q, second_m)
@@ -91,7 +96,17 @@
         copy.start()
         state_loads.append(copy)
 
-    pl.semaphore_wait(barrier, 30)
+    pl.semaphore_wait(barrier, 6 + c)
+
+    def near_signal(r):
+        for peer in near_z:
+            pl.semaphore_signal(hand.at[r], inc=1, device_id=peer, device_id_type=MESH_ID)
+
+    def near_wait(r):
+        pl.semaphore_wait(hand.at[r], 2)
+
+    def partner_signal():
+        pl.semaphore_signal(hand.at[3], inc=1, device_id={"c": 1 - c}, device_id_type=MESH_ID)
 
     def remote(src, dst, send, recv, axis, coordinate):
         return pltpu.make_async_remote_copy(
@@ -109,45 +124,60 @@
         copy.start()
         started.append(copy)
 
-    source = (grads_q, turned_m)
+    source = (raw_q, turned_m)
+    low, high = pl.ds(0, HALF), pl.ds(HALF, HALF)
+
+    def place(a, k):
+        fi, si = f[a], wrap(s[a] + OFFSETS[k])
+        return wrap(fi + 1), wrap(fi + 3), wrap(fi + 2), si
 
     def rs_copy(a, k, kind):
-        fi, si = f[a], wrap(s[a] + OFFSETS[k])
-        plus, minus, far = wrap(fi + 1), wrap(fi + 3), wrap(fi + 2)
-        src = {
-            RELAY_A: lambda: source[a].at[shard_rows(shard_index(a, far, si), 0, HALF)],
-            RELAY_B: lambda: source[a].at[shard_rows(shard_index(a, far, si), HALF, HALF)],
-            DIRECT_P: lambda: source[a].at[shard_rows(shard_index(a, plus, si))],
-            DIRECT_M: lambda: source[a].at[shard_rows(shard_index(a, minus, si))],
-            FORWARD_A: lambda: relay.at[a, k, 0],
-            FORWARD_B: lambda: relay.at[a, k, 1],
+        plus, minus, far, si = place(a, k)
+
+        def mine(owner, start):
+            return source[a].at[shard_rows(shard_index(a, owner, si), start, HALF)]
+
+        src, dst = {
+            RELAY_A: lambda: (mine(far, 0), relay.at[a, k, 0]),
+            RELAY_B: lambda: (mine(far, HALF), relay.at[a, k, 1]),
+            RAW_P: lambda: (mine(plus, HALF), raw_in.at[a, k, 0]),
+            RAW_M: lambda: (mine(minus, 0), raw_in.at[a, k, 1]),
+            SUM_P: lambda: (sum_out.at[a, k, 0], sum_in.at[a, k, 0]),
+            SUM_M: lambda: (sum_out.at[a, k, 1], sum_in.at[a, k, 1]),
         }[kind]()
-        dst = {
-            RELAY_A: lambda: relay.at[a, k, 0],
-            RELAY_B: lambda: relay.at[a, k, 1],
-            DIRECT_P: lambda: held.at[a, k, 0],
-            DIRECT_M: lambda: held.at[a, k, 1],
-            FORWARD_A: lambda: held.at[a, k, 2, pl.ds(0, HALF)],
-            FORWARD_B: lambda: held.at[a, k, 2, pl.ds(HALF, HALF)],
-        }[kind]()
-        target = plus if kind in (RELAY_A, DIRECT_P, FORWARD_A) else minus
+        target = plus if kind in (RELAY_A, RAW_P, SUM_P) else minus
         return remote(
             src, dst, rs_send.at[a, k, kind], rs_recv.at[a, k, kind], first_axis[a], target
         )
 
     def raw_relay(a, k):
+        if a == 0:
+            query_loads[k].wait()
         go(rs_copy(a, k, RELAY_A))
         go(rs_copy(a, k, RELAY_B))
 
     def raw_direct(a, k):
-        go(rs_copy(a, k, DIRECT_P))
-        go(rs_copy(a, k, DIRECT_M))
-
-    def forward(a, k):
-        rs_copy(a, k, RELAY_A).wait_recv()
-        go(rs_copy(a, k, FORWARD_A))
-        rs_copy(a, k, RELAY_B).wait_recv()
-        go(rs_copy(a, k, FORWARD_B))
+        go(rs_copy(a, k, RAW_P))
+        go(rs_copy(a, k, RAW_M))
+
+    def as_f32(value):
+        return value.astype(jnp.float32)
+
+    def pass_on(a, k):
+        plus, minus, far, si = place(a, k)
+        for side, kind, owner, start in ((0, SUM_P, plus, 0), (1, SUM_M, minus, HALF)):
+            rs_copy(a, k, RELAY_A + side).wait_recv()
+            base = shard_index(a, owner, si) * ROWS + start
+
+            def step(i, carry):
+                at = pl.ds(pl.multiple_of(i * 16, 16), 16)
+                mine = source[a][pl.ds(pl.multiple_of(base + i * 16, 16), 16), :]
+                value = as_f32(mine) + as_f32(relay[a, k, side, at, :])
+                sum_out[a, k, side, at, :] = value.astype(jnp.bfloat16)
+                return carry
+
+            lax.fori_loop(0, HALF // 16, step, 0)
+            go(rs_copy(a, k, kind))
 
     def turn(fi):
         def step(i, carry):
@@ -158,53 +188,60 @@
         lax.fori_loop(0, GROUP // 128, step, 0)
 
     def add_up(a, k):
-        for kind in (DIRECT_P, DIRECT_M, FORWARD_A, FORWARD_B):
+        for kind in (RAW_P, RAW_M, SUM_P, SUM_M):
             rs_copy(a, k, kind).wait_recv()
-        if a == 0:
-            own_loads[k].wait()
         if k == 3:
             state_loads[a].wait()
-        own_base = 0 if a == 0 else shard_index(a, f[a], wrap(s[a] + OFFSETS[k])) * ROWS
-
-        def step(i, carry):
-            at = pl.ds(pl.multiple_of(i * BLOCK, BLOCK), BLOCK)
-            if a == 0:
-                mine = own_q[k, at, :]
-            else:
-                mine = turned_m[pl.ds(pl.multiple_of(own_base + i * BLOCK, BLOCK), BLOCK), :]
-            value = mine.astype(jnp.float32)
-            for j in range(3):
-                value = value + held[a, k, j, at, :].astype(jnp.float32)
-            if k == 3:
-                value = value + state[a, at, :]
-            partial[a, k, at, :] = value
-            return carry
-
-        lax.fori_loop(0, ROWS // BLOCK, step, 0)
-
-    low, high = pl.ds(0, HALF), pl.ds(HALF, HALF)
+        base = shard_index(a, f[a], wrap(s[a] + OFFSETS[k])) * ROWS
+        for h in (0, 1):
+            one = (sum_in, raw_in)[h]
+            two = (raw_in, sum_in)[h]
+
+            def step(i, carry):
+                at = pl.ds(pl.multiple_of(i * 16, 16), 16)
+                here = pl.ds(pl.multiple_of(h * HALF + i * 16, 16), 16)
+                mine = source[a][pl.ds(pl.multiple_of(base + h * HALF + i * 16, 16), 16), :]
+                value = as_f32(mine) + as_f32(one[a, k, 0, at, :]) + as_f32(two[a, k, 1, at, :])
+                if k == 3:
+                    partial[a, 1, here, :] = value + state[a, here, :]
+                elif k == 0:
+                    send_s[a, h, at, :] = value.astype(jnp.bfloat16)
+                elif k == 1:
+                    if h == 0:
+                        partial[a, 0, here, :] = value
+                    else:
+                        send_s[a, 2, at, :] = value.astype(jnp.bfloat16)
+                else:
+                    if h == 0:
+                        send_s[a, 3, at, :] = value.astype(jnp.bfloat16)
+                    else:
+                        partial[a, 0, here, :] = value
+                return carry
+
+            lax.fori_loop(0, HALF // 16, step, 0)
 
     def second_copy(a, kind):
         plus, minus = wrap(s[a] + 1), wrap(s[a] + 3)
-        src, dst, target = {
-            T_A: (partial.at[a, 0, low], t_buf.at[a, 0], plus),
-            T_B: (partial.at[a, 0, high], t_buf.at[a, 1], minus),
-            U_P: (partial.at[a, 1, high], u_buf.at[a, 0], plus),
-            U_M: (partial.at[a, 2, low], u_buf.at[a, 1], minus),
-            V_P: (partial.at[a, 1, low], v_buf.at[a, 0], plus),
-            V_M: (partial.at[a, 2, high], v_buf.at[a, 1], minus),
-        }[kind]
+        dst = (t_buf, u_buf, v_buf)[kind // 2].at[a, kind % 2]
+        target = (plus, minus)[kind % 2]
         return remote(
-            src, dst, second_send.at[a, kind], second_recv.at[a, kind], second_axis[a], target
+            send_s.at[a, kind], dst,
+            second_send.at[a, kind], second_recv.at[a, kind], second_axis[a], target,
         )
 
     def merge_t(a):
-        second_copy(a, T_A).wait_recv()
-        partial[a, 1, 0:HALF, :] = partial[a, 1, 0:HALF, :] + t_buf[a, 0]
-        go(second_copy(a, V_P))
-        second_copy(a, T_B).wait_recv()
-        partial[a, 2, HALF:ROWS, :] = partial[a, 2, HALF:ROWS, :] + t_buf[a, 1]
-        go(second_copy(a, V_M))
+        for side, kind in ((0, V_P), (1, V_M)):
+            second_copy(a, T_A + side).wait_recv()
+
+            def step(i, carry):
+                at = pl.ds(pl.multiple_of(i * 16, 16), 16)
+                here = pl.ds(pl.multiple_of(side * HALF + i * 16, 16), 16)
+                value = partial[a, 0, here, :] + as_f32(t_buf[a, side, at, :])
+                send_s[a, kind, at, :] = value.astype(jnp.bfloat16)
+                return carry
+
+            lax.fori_loop(0, HALF // 16, step, 0)
+            go(second_copy(a, kind))
 
     def squares(value):
         return jnp.sum((value * value).reshape(-1, 8, COLS), axis=0)
@@ -216,42 +253,54 @@
             def step(i, acc):
                 at = pl.ds(pl.multiple_of(i * 16, 16), 16)
                 here = pl.ds(pl.multiple_of(h * HALF + i * 16, 16), 16)
-                total = partial[a, 3, here, :] + one[a, 0, at, :] + two[a, 1, at, :]
-                partial[a, 3, here, :] = total
+                total = partial[a, 1, here, :] + as_f32(one[a, 0, at, :]) + as_f32(two[a, 1, at, :])
+                partial[a, 1, here, :] = total
                 return acc + squares(total)
 
             acc = lax.fori_loop(0, HALF // 16, step, acc)
         return acc
 
-    raw_relay(0, 0)
-    raw_direct(0, 0)
-    raw_relay(0, 1)
-    raw_direct(0, 1)
+    for k in (0, 1):
+        raw_relay(0, k)
+        raw_direct(0, k)
     raw_loads[0].wait()
     turn(wrap(x + 2))
     raw_relay(1, 0)
+    raw_relay(1, 1)
+    near_signal(0)
     raw_loads[1].wait()
     turn(wrap(x + 1))
-    go(rs_copy(1, 0, DIRECT_P))
     raw_loads[2].wait()
     turn(wrap(x + 3))
-    go(rs_copy(1, 0, DIRECT_M))
-    raw_relay(1, 1)
+    raw_direct(1, 0)
     raw_direct(1, 1)
+    for a in (0, 1):
+        pass_on(a, 0)
+        raw_relay(a, 2)
+        raw_direct(a, 2)
+    near_wait(0)
+    near_signal(1)
     raw_loads[3].wait()
     turn(x)
-    for k in (0, 1):
-        for a in (0, 1):
-            forward(a, k)
-            raw_relay(a, k + 2)
-            raw_direct(a, k + 2)
-    for a in (0, 1):
-        forward(a, 2)
+    for a in (0, 1):
+        pass_on(a, 1)
+        raw_relay(a, 3)
+        raw_direct(a, 3)
+    near_wait(1)
+    near_signal(2)
+    for a in (0, 1):
+        pass_on(a, 2)
         add_up(a, 0)
         go(second_copy(a, T_A))
         go(second_copy(a, T_B))
-    for a in (0, 1):
-        forward(a, 3)
+    near_wait(2)
+
+    @pl.when(c == 1)
+    def _():
+        partner_signal()
+
+    for a in (0, 1):
+        pass_on(a, 3)
         add_up(a, 1)
         go(second_copy(a, U_P))
     for a in (0, 1):
@@ -261,9 +310,19 @@
         merge_t(a)
     for a in (0, 1):
         add_up(a, 3)
+
+    @pl.when(c == 0)
+    def _():
+        pl.semaphore_wait(hand.at[3], 1)
+        partner_signal()
+
     acc = jnp.zeros((8, COLS), jnp.float32)
     for a in (0, 1):
         acc = finish(a, acc)
+
+    @pl.when(c == 1)
+    def _():
+        pl.semaphore_wait(hand.at[3], 1)
 
     def exchange(stage, row, buf, me, peers):
         row_buf[stage] = row
@@ -308,7 +367,7 @@
 
         def step(i, carry):
             at = pl.ds(pl.multiple_of(i * BLOCK, BLOCK), BLOCK)
-            scaled = clip * partial[a, 3, at, :]
+            scaled = clip * partial[a, 1, at, :]
             master = state[2 + a, at, :]
             first = BETA_ONE * state[4 + a, at, :] + (1.0 - BETA_ONE) * scaled
             variance = BETA_TWO * state[6 + a, at, :] + (1.0 - BETA_TWO) * scaled * scaled
@@ -456,13 +515,16 @@
         scratch_shapes=[
             pltpu.VMEM((COLS, FULL), bf16),
             pltpu.VMEM((FULL, COLS), bf16),
-            pltpu.VMEM((N, ROWS, COLS), bf16),
-            pltpu.VMEM((2, N, 3, ROWS, COLS), bf16),
+            pltpu.VMEM((FULL, COLS), bf16),
             pltpu.VMEM((2, N, 2, HALF, COLS), bf16),
-            pltpu.VMEM((2, N, ROWS, COLS), f32),
-            pltpu.VMEM((2, 2, HALF, COLS), f32),
-            pltpu.VMEM((2, 2, HALF, COLS), f32),
-            pltpu.VMEM((2, 2, HALF, COLS), f32),
+            pltpu.VMEM((2, N, 2, HALF, COLS), bf16),
+            pltpu.VMEM((2, N, 2, HALF, COLS), bf16),
+            pltpu.VMEM((2, N, 2, HALF, COLS), bf16),
+            pltpu.VMEM((2, 2, ROWS, COLS), f32),
+            pltpu.VMEM((2, 6, HALF, COLS), bf16),
+            pltpu.VMEM((2, 2, HALF, COLS), bf16),
+            pltpu.VMEM((2, 2, HALF, COLS), bf16),
+            pltpu.VMEM((2, 2, HALF, COLS), bf16),
             pltpu.VMEM((8, ROWS, COLS), f32),
             pltpu.VMEM((FULL, COLS), bf16),
             pltpu.VMEM((16, 1, 128), f32),
@@ -477,6 +539,7 @@
             pltpu.SemaphoreType.DMA((2, 5, 4)),
             pltpu.SemaphoreType.DMA((2, 15)),
             pltpu.SemaphoreType.DMA((2, 15)),
+            pltpu.SemaphoreType.REGULAR((4,)),
         ],
         compiler_params=pltpu.CompilerParams(
             collective_id=0, has_side_effects=True, vmem_limit_bytes=32 * 2**20

time: 78.7 us -> 69.6 us (0.88)
  Pallas kernels: 76.9 us -> 67.9 us
    pallas_call x1, Pallas kernels: 74.5 us -> 65.5 us  [on_device(): pl.pallas_call(kernel, name='adamw_step', out_shape=[pltpu.VMEM((FULL, CO...]
where the time goes in v3:
time: 69.6 us; the launch traced here: 68.5 us
  Pallas kernels  67.9 us (98%)
    pallas_call x1, Pallas kernels, on_device(): pl.pallas_call(kernel, name='adamw_step', out_shape=[pltpu.VMEM((FULL, CO...  65.5 us
    pallas_call x1, Pallas kernels, on_device(): pl.pallas_call(write_out, name='write_out', out_shape=[jax.ShapeDtypeStru...  2.33 us

profile of v3, /device:TPU:8, one launch (start us, length us, event | category | flops | bytes accessed | tf_op | source)
XLA Modules:
  0.0 68.5 jit_solution(1139063530347306937)
XLA Ops:
  0.6 65.5 %adamw_step.1 = (bf16[3584,256]{1,0:T(8,128)(2,1)S(1)}, bf16[256,3584]{1,0:T(8,128)(2,1)S(1)}, f32[224,256]{1,0:T(8,128)S(1)}, f32[224,256]{1,0:T(8,128)S(1)}, f...) custom-call(bf16[3584,256]{1,0:T(8,128)(2,1)} %bitcast.32, ...), custom_call_target="tpu_custom_call" | custom-call | tf_op jit(solution)/shard_map/adamw_step/pallas_call | solution.py:505
  66.2 2.3 %write_out.1 = (bf16[3584,256]{1,0:T(8,128)(2,1)}, bf16[256,3584]{1,0:T(8,128)(2,1)}, f32[224,256]{1,0:T(8,128)}, f32[224,256]{1,0:T(8,128)}, f32[224,256]{1,0:T...) custom-call(bf16[3584,256]{1,0:T(8,128)(2,1)S(1)} %get-tuple-element.24.refs_0_, ...), custom_call_target="tpu_custom_call" | custom-call | tf_op jit(solution)/shard_map/write_out/pallas_call | solution.py:548

commit v4 on v3

--- a/solution.py
+++ b/solution.py
@@ -32,6 +32,12 @@
     return lax.rem(value, N)
 
 
+def each_block(count, step, carry):
+    for i in range(count):
+        carry = step(i, carry)
+    return carry
+
+
 def shard_rows(index, start=0, size=ROWS):
     return pl.ds(pl.multiple_of(index * ROWS + start, 16), size)
 
@@ -41,7 +47,7 @@
     weight_q, weight_m, shard_q, shard_m, first_q, first_m, variance_q, variance_m,
     raw_m, turned_m, raw_q, relay, raw_in, sum_in, sum_out, partial, send_s, t_buf, u_buf, v_buf, state, gather_m,
     plane_buf, column_buf, row_buf,
-    load_sem, rs_send, rs_recv, second_send, second_recv, ag_send, ag_recv, ar_send, ar_recv, hand,
+    load_sem, rs_send, rs_recv, second_recv, ag_send, ag_recv, ar_send, ar_recv, hand,
 ):
     x, y = lax.axis_index("x"), lax.axis_index("y")
     z, c = lax.axis_index("z"), lax.axis_index("c")
@@ -92,7 +98,7 @@
     for i, ref in enumerate(
         (accum_q, accum_m, master_q, master_m, moment_q, moment_m, second_q, second_m)
     ):
-        copy = pltpu.make_async_copy(ref, state.at[i], load_sem.at[8 + i])
+        copy = pltpu.make_async_copy(ref, state.at[i], load_sem.at[8 + min(i, 2)])
         copy.start()
         state_loads.append(copy)
 
@@ -118,11 +124,8 @@
             device_id_type=MESH_ID,
         )
 
-    started = []
-
     def go(copy):
         copy.start()
-        started.append(copy)
 
     source = (raw_q, turned_m)
     low, high = pl.ds(0, HALF), pl.ds(HALF, HALF)
@@ -147,8 +150,11 @@
         }[kind]()
         target = plus if kind in (RELAY_A, RAW_P, SUM_P) else minus
         return remote(
-            src, dst, rs_send.at[a, k, kind], rs_recv.at[a, k, kind], first_axis[a], target
+            src, dst, rs_send.at[a], rs_recv.at[a, k, min(kind, 2)], first_axis[a], target
         )
+
+    def wait_bytes(ref, sem):
+        pltpu.make_async_copy(ref, ref, sem).wait()
 
     def raw_relay(a, k):
         if a == 0:
@@ -170,13 +176,13 @@
             base = shard_index(a, owner, si) * ROWS + start
 
             def step(i, carry):
-                at = pl.ds(pl.multiple_of(i * 16, 16), 16)
+                at = pl.ds(i * 16, 16)
                 mine = source[a][pl.ds(pl.multiple_of(base + i * 16, 16), 16), :]
                 value = as_f32(mine) + as_f32(relay[a, k, side, at, :])
                 sum_out[a, k, side, at, :] = value.astype(jnp.bfloat16)
                 return carry
 
-            lax.fori_loop(0, HALF // 16, step, 0)
+            each_block(HALF // 16, step, 0)
             go(rs_copy(a, k, kind))
 
     def turn(fi):
@@ -188,8 +194,7 @@
         lax.fori_loop(0, GROUP // 128, step, 0)
 
     def add_up(a, k):
-        for kind in (RAW_P, RAW_M, SUM_P, SUM_M):
-            rs_copy(a, k, kind).wait_recv()
+        wait_bytes(source[a].at[pl.ds(0, 2 * ROWS)], rs_recv.at[a, k, 2])
         if k == 3:
             state_loads[a].wait()
         base = shard_index(a, f[a], wrap(s[a] + OFFSETS[k])) * ROWS
@@ -198,8 +203,8 @@
             two = (raw_in, sum_in)[h]
 
             def step(i, carry):
-                at = pl.ds(pl.multiple_of(i * 16, 16), 16)
-                here = pl.ds(pl.multiple_of(h * HALF + i * 16, 16), 16)
+                at = pl.ds(i * 16, 16)
+                here = pl.ds(h * HALF + i * 16, 16)
                 mine = source[a][pl.ds(pl.multiple_of(base + h * HALF + i * 16, 16), 16), :]
                 value = as_f32(mine) + as_f32(one[a, k, 0, at, :]) + as_f32(two[a, k, 1, at, :])
                 if k == 3:
@@ -218,7 +223,7 @@
                         partial[a, 0, here, :] = value
                 return carry
 
-            lax.fori_loop(0, HALF // 16, step, 0)
+            each_block(HALF // 16, step, 0)
 
     def second_copy(a, kind):
         plus, minus = wrap(s[a] + 1), wrap(s[a] + 3)
@@ -226,7 +231,7 @@
         target = (plus, minus)[kind % 2]
         return remote(
             send_s.at[a, kind], dst,
-            second_send.at[a, kind], second_recv.at[a, kind], second_axis[a], target,
+            rs_send.at[a], second_recv.at[a, min(kind, 2)], second_axis[a], target,
         )
 
     def merge_t(a):
@@ -234,35 +239,35 @@
             second_copy(a, T_A + side).wait_recv()
 
             def step(i, carry):
-                at = pl.ds(pl.multiple_of(i * 16, 16), 16)
-                here = pl.ds(pl.multiple_of(side * HALF + i * 16, 16), 16)
+                at = pl.ds(i * 16, 16)
+                here = pl.ds(side * HALF + i * 16, 16)
                 value = partial[a, 0, here, :] + as_f32(t_buf[a, side, at, :])
                 send_s[a, kind, at, :] = value.astype(jnp.bfloat16)
                 return carry
 
-            lax.fori_loop(0, HALF // 16, step, 0)
+            each_block(HALF // 16, step, 0)
             go(second_copy(a, kind))
 
     def squares(value):
         return jnp.sum((value * value).reshape(-1, 8, COLS), axis=0)
 
     def finish(a, acc):
-        for kind in (U_P, U_M, V_P, V_M):
-            second_copy(a, kind).wait_recv()
+        wait_bytes(source[a].at[pl.ds(0, 2 * ROWS)], second_recv.at[a, 2])
         for h, one, two in ((0, v_buf, u_buf), (1, u_buf, v_buf)):
             def step(i, acc):
-                at = pl.ds(pl.multiple_of(i * 16, 16), 16)
-                here = pl.ds(pl.multiple_of(h * HALF + i * 16, 16), 16)
+                at = pl.ds(i * 16, 16)
+                here = pl.ds(h * HALF + i * 16, 16)
                 total = partial[a, 1, here, :] + as_f32(one[a, 0, at, :]) + as_f32(two[a, 1, at, :])
                 partial[a, 1, here, :] = total
                 return acc + squares(total)
 
-            acc = lax.fori_loop(0, HALF // 16, step, acc)
+            acc = each_block(HALF // 16, step, acc)
         return acc
 
-    for k in (0, 1):
-        raw_relay(0, k)
-        raw_direct(0, k)
+    raw_relay(0, 0)
+    raw_relay(0, 1)
+    raw_direct(0, 0)
+    raw_relay(0, 2)
     raw_loads[0].wait()
     turn(wrap(x + 2))
     raw_relay(1, 0)
@@ -273,26 +278,33 @@
     raw_loads[2].wait()
     turn(wrap(x + 3))
     raw_direct(1, 0)
-    raw_direct(1, 1)
-    for a in (0, 1):
-        pass_on(a, 0)
-        raw_relay(a, 2)
-        raw_direct(a, 2)
+    raw_relay(1, 2)
+    for k in (0, 1):
+        for a in (0, 1):
+            pass_on(a, k)
+            raw_direct(a, k + 1)
     near_wait(0)
     near_signal(1)
     raw_loads[3].wait()
     turn(x)
     for a in (0, 1):
-        pass_on(a, 1)
-        raw_relay(a, 3)
-        raw_direct(a, 3)
-    near_wait(1)
-    near_signal(2)
-    for a in (0, 1):
         pass_on(a, 2)
+    for a in (0, 1):
         add_up(a, 0)
         go(second_copy(a, T_A))
         go(second_copy(a, T_B))
+    near_wait(1)
+    near_signal(2)
+    for a in (0, 1):
+        add_up(a, 1)
+        go(second_copy(a, U_P))
+        raw_relay(a, 3)
+        raw_direct(a, 3)
+    for a in (0, 1):
+        add_up(a, 2)
+        go(second_copy(a, U_M))
+    for a in (0, 1):
+        merge_t(a)
     near_wait(2)
 
     @pl.when(c == 1)
@@ -301,21 +313,15 @@
 
     for a in (0, 1):
         pass_on(a, 3)
-        add_up(a, 1)
-        go(second_copy(a, U_P))
-    for a in (0, 1):
-        add_up(a, 2)
-        go(second_copy(a, U_M))
-    for a in (0, 1):
-        merge_t(a)
-    for a in (0, 1):
-        add_up(a, 3)
 
     @pl.when(c == 0)
     def _():
         pl.semaphore_wait(hand.at[3], 1)
         partner_signal()
 
+    for a in (0, 1):
+        add_up(a, 3)
+
     acc = jnp.zeros((8, COLS), jnp.float32)
     for a in (0, 1):
         acc = finish(a, acc)
@@ -327,26 +333,18 @@
     def exchange(stage, row, buf, me, peers):
         row_buf[stage] = row
         buf[me] = row
-        for d, peer in enumerate(peers):
-            copy = pltpu.make_async_remote_copy(
-                src_ref=row_buf.at[stage],
-                dst_ref=buf.at[me],
-                send_sem=ar_send.at[stage, d],
-                recv_sem=ar_recv.at[stage, d],
-                device_id=peer,
-                device_id_type=MESH_ID,
+        for peer in peers:
+            go(
+                pltpu.make_async_remote_copy(
+                    src_ref=row_buf.at[stage],
+                    dst_ref=buf.at[me],
+                    send_sem=ar_send.at[stage],
+                    recv_sem=ar_recv.at[stage],
+                    device_id=peer,
+                    device_id_type=MESH_ID,
+                )
             )
-            go(copy)
-        for d in range(15):
-            sender = lax.rem(me + 15 - d, 16)
-            pltpu.make_async_remote_copy(
-                src_ref=row_buf.at[stage],
-                dst_ref=buf.at[sender],
-                send_sem=ar_send.at[stage, d],
-                recv_sem=ar_recv.at[stage, d],
-                device_id=peers[d],
-                device_id_type=MESH_ID,
-            ).wait_recv()
+        wait_bytes(buf.at[pl.ds(0, 15)], ar_recv.at[stage])
         return jnp.sum(buf[...], axis=0)
 
     row = jnp.sum(acc, axis=0, keepdims=True)
@@ -358,15 +356,14 @@
 
     gathered = (weight_q, gather_m)
     outs = ((shard_q, first_q, variance_q), (shard_m, first_m, variance_m))
-    for copy in state_loads[2:]:
-        copy.wait()
+    pltpu.make_async_copy(state.at[pl.ds(2, 6)], state.at[pl.ds(2, 6)], load_sem.at[10]).wait()
 
     def update(a):
         base = shard_index(a, f[a], s[a]) * ROWS
         shard_out, first_out, variance_out = outs[a]
 
         def step(i, carry):
-            at = pl.ds(pl.multiple_of(i * BLOCK, BLOCK), BLOCK)
+            at = pl.ds(i * BLOCK, BLOCK)
             scaled = clip * partial[a, 1, at, :]
             master = state[2 + a, at, :]
             first = BETA_ONE * state[4 + a, at, :] + (1.0 - BETA_ONE) * scaled
@@ -386,7 +383,7 @@
             )
             return carry
 
-        lax.fori_loop(0, ROWS // BLOCK, step, 0)
+        each_block(ROWS // BLOCK, step, 0)
 
     ITEMS = (0, 3, 1, 2)
 
@@ -403,23 +400,18 @@
         start, size = {0: (0, ROWS), 1: (0, ROWS), 2: (0, HALF), 3: (HALF, HALF)}[kind]
         ref = gathered[a].at[shard_rows(index, start, size)]
         target = wrap(here + 1) if kind in (0, 2) else wrap(here + 3)
-        return remote(ref, ref, ag_send.at[a, item, kind], ag_recv.at[a, item, kind], axis, target)
+        if kind < 2:
+            slot = 2 * item + kind
+        else:
+            slot = 10 if item == 0 else 11
+        return remote(ref, ref, ag_send.at[a], ag_recv.at[a, slot], axis, target)
 
     def ag_wait(a, item, kind):
-        if item == 0:
-            axis, here = second_axis[a], s[a]
-        else:
-            axis, here = first_axis[a], f[a]
-        owner = {0: wrap(here + 3), 1: wrap(here + 1), 2: wrap(here + 2), 3: wrap(here + 2)}[kind]
-        if item == 0:
-            index = shard_index(a, f[a], owner)
-        else:
-            index = shard_index(a, owner, wrap(s[a] + ITEMS[item - 1]))
-        start, size = {0: (0, ROWS), 1: (0, ROWS), 2: (0, HALF), 3: (HALF, HALF)}[kind]
-        ref = gathered[a].at[shard_rows(index, start, size)]
-        remote(
-            ref, ref, ag_send.at[a, item, kind], ag_recv.at[a, item, kind], axis, here
-        ).wait_recv()
+        wait_bytes(gathered[a].at[pl.ds(0, ROWS)], ag_recv.at[a, 2 * item + kind])
+
+    def ag_wait_far(a, along_first):
+        count = N * ROWS if along_first else ROWS
+        wait_bytes(gathered[a].at[pl.ds(0, count)], ag_recv.at[a, 11 if along_first else 10])
 
     def turn_back(fi):
         def step(i, carry):
@@ -434,15 +426,6 @@
         for item in (0, 1):
             go(ag_copy(a, item, 0))
             go(ag_copy(a, item, 1))
-    for a in (0, 1):
-        ag_wait(a, 0, 0)
-        go(ag_copy(a, 0, 2))
-        ag_wait(a, 0, 1)
-        go(ag_copy(a, 0, 3))
-        for item in (2, 3):
-            go(ag_copy(a, item, 0))
-            go(ag_copy(a, item, 1))
-
     def ag_forward(a, item):
         ag_wait(a, item, 0)
         go(ag_copy(a, item, 2))
@@ -450,10 +433,15 @@
         go(ag_copy(a, item, 3))
 
     for a in (0, 1):
+        ag_forward(a, 0)
+    for item in (2, 3):
+        for a in (0, 1):
+            go(ag_copy(a, item, 0))
+            go(ag_copy(a, item, 1))
+    for a in (0, 1):
         ag_forward(a, 1)
     for a in (0, 1):
-        ag_wait(a, 0, 2)
-        ag_wait(a, 0, 3)
+        ag_wait_far(a, False)
         go(ag_copy(a, 4, 0))
         go(ag_copy(a, 4, 1))
     turn_back(x)
@@ -462,13 +450,13 @@
             ag_forward(a, item)
     turn_back(wrap(x + 1))
     turn_back(wrap(x + 3))
-    for item in (1, 2, 3, 4):
-        for a in (0, 1):
-            ag_wait(a, item, 2)
-            ag_wait(a, item, 3)
+    ag_wait_far(1, True)
     turn_back(wrap(x + 2))
-    for copy in started:
-        copy.wait_send()
+    ag_wait_far(0, True)
+    for a in (0, 1):
+        wait_bytes(gathered[a].at[pl.ds(0, 15 * ROWS)], ag_send.at[a])
+        wait_bytes(gathered[a].at[pl.ds(0, 15 * ROWS)], rs_send.at[a])
+        wait_bytes(plane_buf.at[pl.ds(0, 15)], ar_send.at[a])
 
 
 def write_out(*refs):
@@ -530,15 +518,14 @@
             pltpu.VMEM((16, 1, 128), f32),
             pltpu.VMEM((16, 1, 128), f32),
             pltpu.VMEM((2, 1, 128), f32),
-            pltpu.SemaphoreType.DMA((16,)),
-            pltpu.SemaphoreType.DMA((2, N, 6)),
-            pltpu.SemaphoreType.DMA((2, N, 6)),
-            pltpu.SemaphoreType.DMA((2, 6)),
-            pltpu.SemaphoreType.DMA((2, 6)),
-            pltpu.SemaphoreType.DMA((2, 5, 4)),
-            pltpu.SemaphoreType.DMA((2, 5, 4)),
-            pltpu.SemaphoreType.DMA((2, 15)),
-            pltpu.SemaphoreType.DMA((2, 15)),
+            pltpu.SemaphoreType.DMA((11,)),
+            pltpu.SemaphoreType.DMA((2,)),
+            pltpu.SemaphoreType.DMA((2, N, 3)),
+            pltpu.SemaphoreType.DMA((2, 3)),
+            pltpu.SemaphoreType.DMA((2,)),
+            pltpu.SemaphoreType.DMA((2, 12)),
+            pltpu.SemaphoreType.DMA((2,)),
+            pltpu.SemaphoreType.DMA((2,)),
             pltpu.SemaphoreType.REGULAR((4,)),
         ],
         compiler_params=pltpu.CompilerParams(

time: 69.6 us -> 67 us (0.963); the launches traced: 68.5 us -> 66.9 us
  Pallas kernels: 67.9 us -> 66.3 us
    pallas_call x1, Pallas kernels: 65.5 us -> 64 us  [on_device(): pl.pallas_call(kernel, name='adamw_step', out_shape=[pltpu.VMEM((FULL, CO...]
where the time goes in v4:
time: 67 us; the launch traced here: 66.9 us
  Pallas kernels  66.3 us (99%)
    pallas_call x1, Pallas kernels, on_device(): pl.pallas_call(kernel, name='adamw_step', out_shape=[pltpu.VMEM((FULL, CO...  64 us
    pallas_call x1, Pallas kernels, on_device(): pl.pallas_call(write_out, name='write_out', out_shape=[jax.ShapeDtypeStru...  2.33 us

profile of v4, /device:TPU:8, one launch (start us, length us, event | category | flops | bytes accessed | tf_op | source)
XLA Modules:
  0.0 66.9 jit_solution(7732838137881145603)
XLA Ops:
  0.6 64.0 %adamw_step.1 = (bf16[3584,256]{1,0:T(8,128)(2,1)S(1)}, bf16[256,3584]{1,0:T(8,128)(2,1)S(1)}, f32[224,256]{1,0:T(8,128)S(1)}, f32[224,256]{1,0:T(8,128)S(1)}, f...) custom-call(bf16[3584,256]{1,0:T(8,128)(2,1)} %bitcast.32, ...), custom_call_target="tpu_custom_call" | custom-call | tf_op jit(solution)/shard_map/adamw_step/pallas_call | solution.py:493
  64.6 2.3 %write_out.1 = (bf16[3584,256]{1,0:T(8,128)(2,1)}, bf16[256,3584]{1,0:T(8,128)(2,1)}, f32[224,256]{1,0:T(8,128)}, f32[224,256]{1,0:T(8,128)}, f32[224,256]{1,0:T...) custom-call(bf16[3584,256]{1,0:T(8,128)(2,1)S(1)} %get-tuple-element.24.refs_0_, ...), custom_call_target="tpu_custom_call" | custom-call | tf_op jit(solution)/shard_map/write_out/pallas_call | solution.py:535

commit v5 on v4

--- a/solution.py
+++ b/solution.py
@@ -268,6 +268,7 @@
     raw_relay(0, 1)
     raw_direct(0, 0)
     raw_relay(0, 2)
+    raw_direct(0, 1)
     raw_loads[0].wait()
     turn(wrap(x + 2))
     raw_relay(1, 0)
@@ -279,10 +280,12 @@
     turn(wrap(x + 3))
     raw_direct(1, 0)
     raw_relay(1, 2)
-    for k in (0, 1):
-        for a in (0, 1):
-            pass_on(a, k)
-            raw_direct(a, k + 1)
+    raw_direct(1, 1)
+    for a in (0, 1):
+        pass_on(a, 0)
+    for a in (0, 1):
+        pass_on(a, 1)
+        raw_direct(a, 2)
     near_wait(0)
     near_signal(1)
     raw_loads[3].wait()
@@ -293,13 +296,14 @@
         add_up(a, 0)
         go(second_copy(a, T_A))
         go(second_copy(a, T_B))
+        raw_relay(a, 3)
+    for a in (0, 1):
+        raw_direct(a, 3)
     near_wait(1)
     near_signal(2)
     for a in (0, 1):
         add_up(a, 1)
         go(second_copy(a, U_P))
-        raw_relay(a, 3)
-        raw_direct(a, 3)
     for a in (0, 1):
         add_up(a, 2)
         go(second_copy(a, U_M))
@@ -392,22 +396,28 @@
             axis, here = second_axis[a], s[a]
         else:
             axis, here = first_axis[a], f[a]
-        owner = {0: here, 1: here, 2: wrap(here + 3), 3: wrap(here + 1)}[kind]
+        owner = {2: wrap(here + 3), 3: wrap(here + 1)}.get(kind, here)
         if item == 0:
             index = shard_index(a, f[a], owner)
         else:
             index = shard_index(a, owner, wrap(s[a] + ITEMS[item - 1]))
-        start, size = {0: (0, ROWS), 1: (0, ROWS), 2: (0, HALF), 3: (HALF, HALF)}[kind]
+        if item > 0 and kind < 2:
+            start, size = 0, ROWS
+        else:
+            start, size = (HALF if kind in (1, 3, 4) else 0), HALF
         ref = gathered[a].at[shard_rows(index, start, size)]
-        target = wrap(here + 1) if kind in (0, 2) else wrap(here + 3)
+        target = wrap(here + 1) if kind in (0, 2, 4) else wrap(here + 3)
         if kind < 2:
             slot = 2 * item + kind
+        elif kind > 3:
+            slot = 12
         else:
             slot = 10 if item == 0 else 11
         return remote(ref, ref, ag_send.at[a], ag_recv.at[a, slot], axis, target)
 
     def ag_wait(a, item, kind):
-        wait_bytes(gathered[a].at[pl.ds(0, ROWS)], ag_recv.at[a, 2 * item + kind])
+        size = HALF if item == 0 else ROWS
+        wait_bytes(gathered[a].at[pl.ds(0, size)], ag_recv.at[a, 2 * item + kind])
 
     def ag_wait_far(a, along_first):
         count = N * ROWS if along_first else ROWS
@@ -423,9 +433,12 @@
 
     for a in (0, 1):
         update(a)
-        for item in (0, 1):
-            go(ag_copy(a, item, 0))
-            go(ag_copy(a, item, 1))
+        for kind in (0, 1, 4, 5):
+            go(ag_copy(a, 0, kind))
+    for a in (0, 1):
+        go(ag_copy(a, 1, 0))
+        go(ag_copy(a, 1, 1))
+
     def ag_forward(a, item):
         ag_wait(a, item, 0)
         go(ag_copy(a, item, 2))
@@ -434,16 +447,17 @@
 
     for a in (0, 1):
         ag_forward(a, 0)
-    for item in (2, 3):
-        for a in (0, 1):
+    for a in (0, 1):
+        wait_bytes(gathered[a].at[pl.ds(0, ROWS)], ag_recv.at[a, 12])
+        for item in (2, 3):
             go(ag_copy(a, item, 0))
             go(ag_copy(a, item, 1))
-    for a in (0, 1):
-        ag_forward(a, 1)
     for a in (0, 1):
         ag_wait_far(a, False)
         go(ag_copy(a, 4, 0))
         go(ag_copy(a, 4, 1))
+    for a in (0, 1):
+        ag_forward(a, 1)
     turn_back(x)
     for item in (2, 3, 4):
         for a in (0, 1):
@@ -523,7 +537,7 @@
             pltpu.SemaphoreType.DMA((2, N, 3)),
             pltpu.SemaphoreType.DMA((2, 3)),
             pltpu.SemaphoreType.DMA((2,)),
-            pltpu.SemaphoreType.DMA((2, 12)),
+            pltpu.SemaphoreType.DMA((2, 13)),
             pltpu.SemaphoreType.DMA((2,)),
             pltpu.SemaphoreType.DMA((2,)),
             pltpu.SemaphoreType.REGULAR((4,)),

time: 67 us -> 64.8 us (0.967); the launches traced: 66.9 us -> 63.6 us
  Pallas kernels: 66.3 us -> 63 us
    pallas_call x1, Pallas kernels: 64 us -> 60.6 us  [on_device(): pl.pallas_call(kernel, name='adamw_step', out_shape=[pltpu.VMEM((FULL, CO...]
where the time goes in v5:
time: 64.8 us; the launch traced here: 63.6 us
  Pallas kernels  63 us (97%)
    pallas_call x1, Pallas kernels, on_device(): pl.pallas_call(kernel, name='adamw_step', out_shape=[pltpu.VMEM((FULL, CO...  60.6 us
    pallas_call x1, Pallas kernels, on_device(): pl.pallas_call(write_out, name='write_out', out_shape=[jax.ShapeDtypeStru...  2.33 us

profile of v5, /device:TPU:8, one launch (start us, length us, event | category | flops | bytes accessed | tf_op | source)
XLA Modules:
  0.0 63.6 jit_solution(18207531752750338562)
XLA Ops:
  0.6 60.6 %adamw_step.1 = (bf16[3584,256]{1,0:T(8,128)(2,1)S(1)}, bf16[256,3584]{1,0:T(8,128)(2,1)S(1)}, f32[224,256]{1,0:T(8,128)S(1)}, f32[224,256]{1,0:T(8,128)S(1)}, f...) custom-call(bf16[3584,256]{1,0:T(8,128)(2,1)} %bitcast.32, ...), custom_call_target="tpu_custom_call" | custom-call | tf_op jit(solution)/shard_map/adamw_step/pallas_call | solution.py:507
  61.3 2.3 %write_out.1 = (bf16[3584,256]{1,0:T(8,128)(2,1)}, bf16[256,3584]{1,0:T(8,128)(2,1)}, f32[224,256]{1,0:T(8,128)}, f32[224,256]{1,0:T(8,128)}, f32[224,256]{1,0:T...) custom-call(bf16[3584,256]{1,0:T(8,128)(2,1)S(1)} %get-tuple-element.24.refs_0_, ...), custom_call_target="tpu_custom_call" | custom-call | tf_op jit(solution)/shard_map/write_out/pallas_call | solution.py:549

commit v6 on v5

--- a/solution.py
+++ b/solution.py
@@ -57,13 +57,27 @@
     def shard_index(a, fi, si):
         return si * N + fi if a == 0 else fi * N + si
 
-    plane_peers, column_peers = [], []
-    me_plane, me_column = x * N + y, z * 2 + c
-    for d in range(1, 16):
-        peer = lax.rem(me_plane + d, 16)
-        plane_peers.append({"x": peer // N, "y": lax.rem(peer, N), "z": z, "c": c})
-        peer = lax.rem(me_column + d, 16)
-        column_peers.append({"x": x, "y": y, "z": peer // 2, "c": lax.rem(peer, 2)})
+    barrier = pltpu.get_barrier_semaphore()
+    near_z = ({"z": lax.rem(z + 1, 8)}, {"z": lax.rem(z + 7, 8)})
+    for peer in (
+        {"x": wrap(x + 1)}, {"x": wrap(x + 3)}, {"y": wrap(y + 1)}, {"y": wrap(y + 3)}, *near_z
+    ):
+        pl.semaphore_signal(barrier, inc=1, device_id=peer, device_id_type=MESH_ID)
+
+    @pl.when(c == 0)
+    def _():
+        pl.semaphore_signal(barrier, inc=1, device_id={"c": 1}, device_id_type=MESH_ID)
+
+    me_plane = x * N + y
+    near_first = (0, 1, 3, 2)
+    plane_peers = [
+        {"x": wrap(x + dx), "y": wrap(y + dy), "c": 1}
+        for dx in reversed(near_first) for dy in reversed(near_first) if dx + dy > 0
+    ]
+    column_peers = [
+        {"z": lax.rem(z + dz, 8), "c": other}
+        for dz in (4, 3, 5, 2, 6, 1, 7, 0) for other in (0, 1) if dz + 1 - other > 0
+    ]
 
     def group_cols(fi):
         return pl.ds(pl.multiple_of(fi * GROUP, 128), GROUP)
@@ -76,17 +90,6 @@
         )
         copy.start()
         raw_loads.append(copy)
-
-    barrier = pltpu.get_barrier_semaphore()
-    near_z = ({"z": lax.rem(z + 1, 8)}, {"z": lax.rem(z + 7, 8)})
-    for peer in (
-        {"x": wrap(x + 1)}, {"x": wrap(x + 3)}, {"y": wrap(y + 1)}, {"y": wrap(y + 3)}, *near_z
-    ):
-        pl.semaphore_signal(barrier, inc=1, device_id=peer, device_id_type=MESH_ID)
-
-    @pl.when(c == 0)
-    def _():
-        pl.semaphore_signal(barrier, inc=1, device_id={"c": 1}, device_id_type=MESH_ID)
 
     query_loads = []
     for k in range(N):
@@ -102,6 +105,16 @@
         copy.start()
         state_loads.append(copy)
 
+    def turn(fi):
+        def step(i, carry):
+            at = pl.ds(pl.multiple_of(fi * GROUP + i * 128, 128), 128)
+            turned_m[at, :] = raw_m[:, at].T
+            return carry
+
+        lax.fori_loop(0, GROUP // 128, step, 0)
+
+    raw_loads[0].wait()
+    turn(wrap(x + 2))
     pl.semaphore_wait(barrier, 6 + c)
 
     def near_signal(r):
@@ -150,7 +163,7 @@
         }[kind]()
         target = plus if kind in (RELAY_A, RAW_P, SUM_P) else minus
         return remote(
-            src, dst, rs_send.at[a], rs_recv.at[a, k, min(kind, 2)], first_axis[a], target
+            src, dst, rs_send.at[a], rs_recv.at[a, k, 0 if kind < 2 else 1], first_axis[a], target
         )
 
     def wait_bytes(ref, sem):
@@ -171,8 +184,8 @@
 
     def pass_on(a, k):
         plus, minus, far, si = place(a, k)
+        wait_bytes(source[a].at[pl.ds(0, ROWS)], rs_recv.at[a, k, 0])
         for side, kind, owner, start in ((0, SUM_P, plus, 0), (1, SUM_M, minus, HALF)):
-            rs_copy(a, k, RELAY_A + side).wait_recv()
             base = shard_index(a, owner, si) * ROWS + start
 
             def step(i, carry):
@@ -185,16 +198,8 @@
             each_block(HALF // 16, step, 0)
             go(rs_copy(a, k, kind))
 
-    def turn(fi):
-        def step(i, carry):
-            at = pl.ds(pl.multiple_of(fi * GROUP + i * 128, 128), 128)
-            turned_m[at, :] = raw_m[:, at].T
-            return carry
-
-        lax.fori_loop(0, GROUP // 128, step, 0)
-
     def add_up(a, k):
-        wait_bytes(source[a].at[pl.ds(0, 2 * ROWS)], rs_recv.at[a, k, 2])
+        wait_bytes(source[a].at[pl.ds(0, 2 * ROWS)], rs_recv.at[a, k, 1])
         if k == 3:
             state_loads[a].wait()
         base = shard_index(a, f[a], wrap(s[a] + OFFSETS[k])) * ROWS
@@ -231,12 +236,12 @@
         target = (plus, minus)[kind % 2]
         return remote(
             send_s.at[a, kind], dst,
-            rs_send.at[a], second_recv.at[a, min(kind, 2)], second_axis[a], target,
+            rs_send.at[a], second_recv.at[a, 0 if kind < 2 else 1], second_axis[a], target,
         )
 
     def merge_t(a):
+        wait_bytes(source[a].at[pl.ds(0, ROWS)], second_recv.at[a, 0])
         for side, kind in ((0, V_P), (1, V_M)):
-            second_copy(a, T_A + side).wait_recv()
 
             def step(i, carry):
                 at = pl.ds(i * 16, 16)
@@ -252,7 +257,7 @@
         return jnp.sum((value * value).reshape(-1, 8, COLS), axis=0)
 
     def finish(a, acc):
-        wait_bytes(source[a].at[pl.ds(0, 2 * ROWS)], second_recv.at[a, 2])
+        wait_bytes(source[a].at[pl.ds(0, 2 * ROWS)], second_recv.at[a, 1])
         for h, one, two in ((0, v_buf, u_buf), (1, u_buf, v_buf)):
             def step(i, acc):
                 at = pl.ds(i * 16, 16)
@@ -269,8 +274,6 @@
     raw_direct(0, 0)
     raw_relay(0, 2)
     raw_direct(0, 1)
-    raw_loads[0].wait()
-    turn(wrap(x + 2))
     raw_relay(1, 0)
     raw_relay(1, 1)
     near_signal(0)
@@ -334,27 +337,39 @@
     def _():
         pl.semaphore_wait(hand.at[3], 1)
 
-    def exchange(stage, row, buf, me, peers):
-        row_buf[stage] = row
-        buf[me] = row
-        for peer in peers:
-            go(
-                pltpu.make_async_remote_copy(
-                    src_ref=row_buf.at[stage],
-                    dst_ref=buf.at[me],
-                    send_sem=ar_send.at[stage],
-                    recv_sem=ar_recv.at[stage],
-                    device_id=peer,
-                    device_id_type=MESH_ID,
-                )
-            )
-        wait_bytes(buf.at[pl.ds(0, 15)], ar_recv.at[stage])
-        return jnp.sum(buf[...], axis=0)
+    def row_copy(stage, dst, peer):
+        return pltpu.make_async_remote_copy(
+            src_ref=row_buf.at[stage],
+            dst_ref=dst,
+            send_sem=ar_send.at[stage],
+            recv_sem=ar_recv.at[stage],
+            device_id=peer,
+            device_id_type=MESH_ID,
+        )
 
     row = jnp.sum(acc, axis=0, keepdims=True)
     row = row[:, :128] + row[:, 128:]
-    row = exchange(0, row, plane_buf, me_plane, plane_peers)
-    row = exchange(1, row, column_buf, me_column, column_peers)
+    row_buf[0] = row
+    for peer in plane_peers:
+        go(row_copy(0, plane_buf.at[c * 16 + me_plane], peer))
+
+    @pl.when(c == 0)
+    def _():
+        go(row_copy(0, plane_buf.at[c * 16 + me_plane], {"c": 1}))
+        wait_bytes(column_buf, ar_recv.at[1])
+
+    @pl.when(c == 1)
+    def _():
+        plane_buf[16 + me_plane] = row
+        wait_bytes(plane_buf.at[pl.ds(0, 31)], ar_recv.at[0])
+        plane_row = jnp.sum(plane_buf[...], axis=0)
+        row_buf[1] = plane_row
+        column_buf[z] = plane_row
+        for peer in column_peers:
+            go(row_copy(1, column_buf.at[z], peer))
+        wait_bytes(column_buf.at[pl.ds(0, 7)], ar_recv.at[1])
+
+    row = jnp.sum(column_buf[...], axis=0)
     sumsq = jnp.sum(row, axis=1, keepdims=True)
     clip = jnp.minimum(1.0, lax.rsqrt(sumsq / float(ENTRIES) + 1e-06))
 
@@ -408,28 +423,25 @@
         ref = gathered[a].at[shard_rows(index, start, size)]
         target = wrap(here + 1) if kind in (0, 2, 4) else wrap(here + 3)
         if kind < 2:
-            slot = 2 * item + kind
+            slot = item
         elif kind > 3:
-            slot = 12
+            slot = 5
+        elif item == 0:
+            slot = 6
         else:
-            slot = 10 if item == 0 else 11
+            slot = 8 if item == 4 else 7
         return remote(ref, ref, ag_send.at[a], ag_recv.at[a, slot], axis, target)
 
-    def ag_wait(a, item, kind):
-        size = HALF if item == 0 else ROWS
-        wait_bytes(gathered[a].at[pl.ds(0, size)], ag_recv.at[a, 2 * item + kind])
-
-    def ag_wait_far(a, along_first):
-        count = N * ROWS if along_first else ROWS
-        wait_bytes(gathered[a].at[pl.ds(0, count)], ag_recv.at[a, 11 if along_first else 10])
-
-    def turn_back(fi):
+    def ag_wait(a, slot, shards):
+        wait_bytes(gathered[a].at[pl.ds(0, shards * ROWS)], ag_recv.at[a, slot])
+
+    def turn_back(fi, count=GROUP // 128, tile=0):
         def step(i, carry):
-            at = pl.ds(pl.multiple_of(fi * GROUP + i * 128, 128), 128)
+            at = pl.ds(pl.multiple_of(fi * GROUP + lax.rem(tile + i, 7) * 128, 128), 128)
             weight_m[:, at] = gather_m[at, :].T
             return carry
 
-        lax.fori_loop(0, GROUP // 128, step, 0)
+        lax.fori_loop(0, count, step, 0)
 
     for a in (0, 1):
         update(a)
@@ -440,20 +452,19 @@
         go(ag_copy(a, 1, 1))
 
     def ag_forward(a, item):
-        ag_wait(a, item, 0)
+        ag_wait(a, item, 1 if item == 0 else 2)
         go(ag_copy(a, item, 2))
-        ag_wait(a, item, 1)
         go(ag_copy(a, item, 3))
 
     for a in (0, 1):
         ag_forward(a, 0)
     for a in (0, 1):
-        wait_bytes(gathered[a].at[pl.ds(0, ROWS)], ag_recv.at[a, 12])
+        ag_wait(a, 5, 1)
         for item in (2, 3):
             go(ag_copy(a, item, 0))
             go(ag_copy(a, item, 1))
     for a in (0, 1):
-        ag_wait_far(a, False)
+        ag_wait(a, 6, 1)
         go(ag_copy(a, 4, 0))
         go(ag_copy(a, 4, 1))
     for a in (0, 1):
@@ -464,13 +475,26 @@
             ag_forward(a, item)
     turn_back(wrap(x + 1))
     turn_back(wrap(x + 3))
-    ag_wait_far(1, True)
-    turn_back(wrap(x + 2))
-    ag_wait_far(0, True)
+    ag_wait(1, 7, 3)
+    across = wrap(y + 2)
+    window = across * 7 // 4 - across // 3
+    turn_back(wrap(x + 2), 4, window + 3)
+    ag_wait(1, 8, 1)
+    turn_back(wrap(x + 2), 3, window)
+    ag_wait(0, 7, 3)
+    ag_wait(0, 8, 1)
     for a in (0, 1):
         wait_bytes(gathered[a].at[pl.ds(0, 15 * ROWS)], ag_send.at[a])
         wait_bytes(gathered[a].at[pl.ds(0, 15 * ROWS)], rs_send.at[a])
-        wait_bytes(plane_buf.at[pl.ds(0, 15)], ar_send.at[a])
+
+    @pl.when(c == 0)
+    def _():
+        wait_bytes(plane_buf.at[pl.ds(0, 16)], ar_send.at[0])
+
+    @pl.when(c == 1)
+    def _():
+        wait_bytes(plane_buf.at[pl.ds(0, 15)], ar_send.at[0])
+        wait_bytes(plane_buf.at[pl.ds(0, 15)], ar_send.at[1])
 
 
 def write_out(*refs):
@@ -529,15 +553,15 @@
             pltpu.VMEM((2, 2, HALF, COLS), bf16),
             pltpu.VMEM((8, ROWS, COLS), f32),
             pltpu.VMEM((FULL, COLS), bf16),
-            pltpu.VMEM((16, 1, 128), f32),
-            pltpu.VMEM((16, 1, 128), f32),
+            pltpu.VMEM((32, 1, 128), f32),
+            pltpu.VMEM((8, 1, 128), f32),
             pltpu.VMEM((2, 1, 128), f32),
             pltpu.SemaphoreType.DMA((11,)),
             pltpu.SemaphoreType.DMA((2,)),
-            pltpu.SemaphoreType.DMA((2, N, 3)),
-            pltpu.SemaphoreType.DMA((2, 3)),
+            pltpu.SemaphoreType.DMA((2, N, 2)),
+            pltpu.SemaphoreType.DMA((2, 2)),
             pltpu.SemaphoreType.DMA((2,)),
-            pltpu.SemaphoreType.DMA((2, 13)),
+            pltpu.SemaphoreType.DMA((2, 9)),
             pltpu.SemaphoreType.DMA((2,)),
             pltpu.SemaphoreType.DMA((2,)),
             pltpu.SemaphoreType.REGULAR((4,)),

time: 64.8 us -> 63.1 us (0.974)
  the two profiles are of different devices: /device:TPU:8 before, /device:TPU:1 now
where the time goes in v6:
time: 63.1 us; the launch traced here: 63 us
  Pallas kernels  62.4 us (99%)
  between operations  0.64 us (1%)
    pallas_call x1, Pallas kernels, on_device(): pl.pallas_call(kernel, name='adamw_step', out_shape=[pltpu.VMEM((FULL, CO...  60 us
    pallas_call x1, Pallas kernels, on_device(): pl.pallas_call(write_out, name='write_out', out_shape=[jax.ShapeDtypeStru...  2.33 us

profile of v6, /device:TPU:1, one launch (start us, length us, event | category | flops | bytes accessed | tf_op | source)
XLA Modules:
  0.0 63.0 jit_solution(13290802619772460300)
XLA Ops:
  0.6 60.0 %adamw_step.1 = (bf16[3584,256]{1,0:T(8,128)(2,1)S(1)}, bf16[256,3584]{1,0:T(8,128)(2,1)S(1)}, f32[224,256]{1,0:T(8,128)S(1)}, f32[224,256]{1,0:T(8,128)S(1)}, f...) custom-call(bf16[3584,256]{1,0:T(8,128)(2,1)} %bitcast.32, ...), custom_call_target="tpu_custom_call" | custom-call | tf_op jit(solution)/shard_map/adamw_step/pallas_call | solution.py:531
  60.7 2.3 %write_out.1 = (bf16[3584,256]{1,0:T(8,128)(2,1)}, bf16[256,3584]{1,0:T(8,128)(2,1)}, f32[224,256]{1,0:T(8,128)}, f32[224,256]{1,0:T(8,128)}, f32[224,256]{1,0:T...) custom-call(bf16[3584,256]{1,0:T(8,128)(2,1)S(1)} %get-tuple-element.24.refs_0_, ...), custom_call_target="tpu_custom_call" | custom-call | tf_op jit(solution)/shard_map/write_out/pallas_call | solution.py:573

commit v7 on v6

--- a/solution.py
+++ b/solution.py
@@ -82,21 +82,16 @@
     def group_cols(fi):
         return pl.ds(pl.multiple_of(fi * GROUP, 128), GROUP)
 
-    raw_loads = []
-    for d in (2, 1, 3, 0):
-        fi = wrap(x + d)
-        copy = pltpu.make_async_copy(
-            grads_m.at[:, group_cols(fi)], raw_m.at[:, group_cols(fi)], load_sem.at[d]
-        )
-        copy.start()
-        raw_loads.append(copy)
-
-    query_loads = []
-    for k in range(N):
+    raw_loads, query_loads = [], []
+    for k, d in enumerate((2, 1, 3, 0)):
         rows = pl.ds(pl.multiple_of(wrap(x + OFFSETS[k]) * GROUP, GROUP), GROUP)
         copy = pltpu.make_async_copy(grads_q.at[rows], raw_q.at[rows], load_sem.at[4 + k])
         copy.start()
         query_loads.append(copy)
+        cols = group_cols(wrap(x + d))
+        copy = pltpu.make_async_copy(grads_m.at[:, cols], raw_m.at[:, cols], load_sem.at[d])
+        copy.start()
+        raw_loads.append(copy)
     state_loads = []
     for i, ref in enumerate(
         (accum_q, accum_m, master_q, master_m, moment_q, moment_m, second_q, second_m)
@@ -295,11 +290,11 @@
     turn(x)
     for a in (0, 1):
         pass_on(a, 2)
+        raw_relay(a, 3)
     for a in (0, 1):
         add_up(a, 0)
         go(second_copy(a, T_A))
         go(second_copy(a, T_B))
-        raw_relay(a, 3)
     for a in (0, 1):
         raw_direct(a, 3)
     near_wait(1)
@@ -311,15 +306,14 @@
         add_up(a, 2)
         go(second_copy(a, U_M))
     for a in (0, 1):
+        pass_on(a, 3)
+    for a in (0, 1):
         merge_t(a)
     near_wait(2)
 
     @pl.when(c == 1)
     def _():
         partner_signal()
-
-    for a in (0, 1):
-        pass_on(a, 3)
 
     @pl.when(c == 0)
     def _():
@@ -500,13 +494,15 @@
 def write_out(*refs):
     sources, targets, sem = refs[:8], refs[8:16], refs[16]
     copies = [
-        pltpu.make_async_copy(source, target, sem.at[i])
+        pltpu.make_async_copy(source, target, sem.at[min(i, 2)])
         for i, (source, target) in enumerate(zip(sources, targets))
     ]
     for copy in copies:
         copy.start()
-    for copy in copies:
+    for copy in copies[:2]:
         copy.wait()
+    whole = sources[0].at[pl.ds(0, 12 * ROWS)]
+    pltpu.make_async_copy(whole, whole, sem.at[2]).wait()
 
 
 def on_device(
@@ -576,7 +572,7 @@
         out_shape=[jax.ShapeDtypeStruct(out.shape, out.dtype) for out in outs],
         in_specs=[pl.BlockSpec(memory_space=pltpu.VMEM)] * 8,
         out_specs=[hbm_spec] * 8,
-        scratch_shapes=[pltpu.SemaphoreType.DMA((8,))],
+        scratch_shapes=[pltpu.SemaphoreType.DMA((3,))],
         compiler_params=pltpu.CompilerParams(vmem_limit_bytes=2**20),
     )(*outs)
     weight_q, weight_m, shard_q, shard_m, first_q, first_m, variance_q, variance_m = outs

time: 63.1 us -> 62.7 us (level)
  the two profiles are of different devices: /device:TPU:1 before, /device:TPU:8 now
where the time goes in v7:
time: 62.7 us; the launch traced here: 61.5 us
  Pallas kernels  60.9 us (97%)
  between operations  0.64 us (1%)
    pallas_call x1, Pallas kernels, on_device(): pl.pallas_call(kernel, name='adamw_step', out_shape=[pltpu.VMEM((FULL, CO...  58.6 us
    pallas_call x1, Pallas kernels, on_device(): pl.pallas_call(write_out, name='write_out', out_shape=[jax.ShapeDtypeStru...  2.29 us

profile of v7, /device:TPU:8, one launch (start us, length us, event | category | flops | bytes accessed | tf_op | source)
XLA Modules:
  0.0 61.5 jit_solution(9170362228101087437)
XLA Ops:
  0.6 58.6 %adamw_step.1 = (bf16[3584,256]{1,0:T(8,128)(2,1)S(1)}, bf16[256,3584]{1,0:T(8,128)(2,1)S(1)}, f32[224,256]{1,0:T(8,128)S(1)}, f32[224,256]{1,0:T(8,128)S(1)}, f...) custom-call(bf16[3584,256]{1,0:T(8,128)(2,1)} %bitcast.32, ...), custom_call_target="tpu_custom_call" | custom-call | tf_op jit(solution)/shard_map/adamw_step/pallas_call | solution.py:527
  59.2 2.3 %write_out.1 = (bf16[3584,256]{1,0:T(8,128)(2,1)}, bf16[256,3584]{1,0:T(8,128)(2,1)}, f32[224,256]{1,0:T(8,128)}, f32[224,256]{1,0:T(8,128)}, f32[224,256]{1,0:T...) custom-call(bf16[3584,256]{1,0:T(8,128)(2,1)S(1)} %get-tuple-element.24.refs_0_, ...), custom_call_target="tpu_custom_call" | custom-call | tf_op jit(solution)/shard_map/write_out/pallas_call | solution.py:569
